TPU v7x, 256 devices: a whole 4x4x8 slice. The times are simulated.
256 devices in a mesh: ctx: 16 (over z, core), grp: 16 (over x, y).
Axes of the slice: x: 4, y: 4, z: 8, core: 2. Of those that a mesh axis runs over, the one named last changes fastest.
Arguments:
- queries: bfloat16 [4096, 8192], P('ctx', 'grp'), may hold values from -27 to 27, as said below
- keys: bfloat16 [4096, 1024], P('ctx'), may hold values from -27 to 27
- values: bfloat16 [4096, 1024], P('ctx'), may hold values from -6 to 6
- out_weight: bfloat16 [8192, 8192], P('grp'), may hold values from -0.0625 to 0.0625
- span_order: int32 [32], replicated, may hold values from 0 to 31, each once
- document: int32 [4096], replicated, may hold values from 0 to 3, never falling along the last dimension, each value on 1 to 2048 neighbouring positions
Outputs:
- projected: bfloat16 [4096, 8192], P('ctx', 'grp')
Inputs may be any that keep to these rules, and one draw needn't show every extreme that they name: `queries`: queries and keys are of order one, except a few rows that may be larger.
All inputs are finite; a program needn't handle non-finite values.
Results may differ from a plain program's by a relative error of at most 0.023.
Values may be sent and summed in bfloat16 or wider, within the bound.
No kernel may reach another device: no remote copies, remote signals or barrier semaphores. Data moves between devices by JAX's collectives and lax.ppermute only.
A program may use at most 128 MiB of HBM per device.

v0:
```python
import math

import jax
import jax.numpy as jnp
from jax import lax
from jax.sharding import PartitionSpec as P

HEAD_DIM = 128
QUERY_GROUP = 8


def in_one_piece(arrays, axis, dim, along):
    ends, at = ([], 0)
    for a in arrays[:-1]:
        at += a.shape[along]
        ends.append(at)
    both = jnp.concatenate(arrays, axis=along)
    return tuple(jnp.split(lax.all_gather(both, axis, axis=dim, tiled=True), ends, axis=along))


def cut_along(x, dim, count):
    shape = x.shape
    parts = x.reshape(*shape[:dim], count, shape[dim] // count, *shape[dim + 1 :])
    return jnp.moveaxis(parts, dim, 0)


def summed_on_arrival(x, axis, dim):
    parts = cut_along(x, dim, lax.axis_size(axis))
    arrived = lax.all_to_all(parts, axis, split_axis=0, concat_axis=0, tiled=True)
    return arrived.astype(jnp.float32).sum(axis=0)


def span_positions(span_order, first_row, count, tok_rows):
    rows = first_row + jnp.arange(count, dtype=jnp.int32)
    span_len = tok_rows // 2
    return jnp.take(span_order, rows // span_len) * span_len + rows % span_len


def attend(
    state, query_block, query_pos, query_doc, key_block, value_block, key_pos, key_doc, kv_heads
):
    out_acc, run_max, run_sum = state
    rows = query_block.shape[0]
    count = key_block.shape[0]
    group_size = query_block.shape[1] // (kv_heads * HEAD_DIM)
    grouped = query_block.reshape(rows, kv_heads, group_size, HEAD_DIM)
    key_view = key_block.reshape(count, kv_heads, HEAD_DIM)
    value_view = value_block.reshape(count, kv_heads, HEAD_DIM)
    scores = jnp.einsum("rkgd,skd->kgrs", grouped, key_view, preferred_element_type=jnp.float32)
    scores = scores * (1.0 / math.sqrt(HEAD_DIM))
    visible = (key_pos[None, :] <= query_pos[:, None]) & (key_doc[None, :] == query_doc[:, None])
    scores = jnp.where(visible, scores, -jnp.inf)
    new_max = jnp.max(scores, axis=-1)
    safe_max = jnp.where(new_max == -jnp.inf, 0.0, new_max)
    rescale = jnp.exp(run_max - safe_max)
    probs = jnp.exp(scores - safe_max[..., None])
    new_sum = run_sum * rescale + jnp.sum(probs, axis=-1)
    mixed = jnp.einsum(
        "kgrs,skd->kgrd", probs.astype(jnp.bfloat16), value_view, preferred_element_type=jnp.float32
    )
    return (out_acc * rescale[..., None] + mixed, new_max, new_sum)


def shards(queries, keys, values, out_weight, span_order, document):
    own_index = lax.axis_index("ctx")
    group_index = lax.axis_index("grp")
    tok_rows = queries.shape[0]
    local_heads = queries.shape[1] // HEAD_DIM
    kv_heads = max(1, local_heads // QUERY_GROUP)
    group_size = local_heads // kv_heads
    kv_first = group_index * local_heads // QUERY_GROUP
    key_local = lax.dynamic_slice_in_dim(keys, kv_first * HEAD_DIM, kv_heads * HEAD_DIM, 1)
    value_local = lax.dynamic_slice_in_dim(values, kv_first * HEAD_DIM, kv_heads * HEAD_DIM, 1)
    found = span_positions(span_order, own_index * tok_rows + 0, tok_rows, tok_rows)
    own_doc = jnp.take(document, found)
    start_state = (
        jnp.zeros((kv_heads, group_size, tok_rows, HEAD_DIM), jnp.float32),
        jnp.full((kv_heads, group_size, tok_rows), -jnp.inf, jnp.float32),
        jnp.zeros((kv_heads, group_size, tok_rows), jnp.float32),
    )
    pieces = in_one_piece((key_local, value_local), "ctx", 0, 1)
    count = pieces[0].shape[0]
    key_pos = span_positions(span_order, jnp.int32(0), count, tok_rows)
    key_doc = jnp.take(document, key_pos)
    state = attend(
        start_state, queries, found, own_doc, pieces[0], pieces[1], key_pos, key_doc, kv_heads
    )
    out_acc, run_max, run_sum = state
    attended = (out_acc / run_sum[..., None]).astype(jnp.bfloat16)
    weight_view = out_weight.reshape(kv_heads, group_size, HEAD_DIM, out_weight.shape[1])
    partial_value = jnp.einsum(
        "kgrd,kgdm->rm", attended, weight_view, preferred_element_type=jnp.float32
    )
    return summed_on_arrival(partial_value.astype(jnp.bfloat16), "grp", 1).astype(jnp.bfloat16)


def solution(mesh):
    in_specs = (P("ctx", "grp"), P("ctx", None), P("ctx", None), P("grp", None), P(), P())
    out_specs = P("ctx", "grp")
    return jax.shard_map(shards, mesh=mesh, in_specs=in_specs, out_specs=out_specs, check_vma=False)
```

profile of v0, /device:TPU:96, one launch (start us, length us, event | category | flops | bytes accessed | tf_op | source)
XLA Modules:
  0.0 175.0 jit_solution(3079316423473608644)
XLA Ops:
  6.5 0.0 copy-start
  6.5 0.0 all-gather.2.cloned.1.call-start
  6.5 0.9 constant_dynamic-slice_fusion
  7.5 0.7 pad_maximum_fusion
  8.1 0.0 all-gather.2.cloned.1.call-update
  8.6 1.8 %fusion.47 = (s32[1]{0:T(128)}, s32[1]{0:T(128)}, s32[1]{0:T(128)}, s32[1]{0:T(128)}, s32[1]{0:T(128)}, /*index=5*/s32[1]{0:T(128)}, s32[1]{0:T(128)}, s32[1]{0:...) fusion(s32[32]{0:T(128)} %param.10), kind=kLoop, calls=%fused_computation.147 | loop fusion | bytes 104 | tf_op jit(solution)/shard_map/jit(_take)/gather | solution.py:36
  10.4 2.1 %fusion.46 = (s32[1]{0:T(128)}, s32[1]{0:T(128)}, s32[1]{0:T(128)}, s32[1]{0:T(128)}, s32[1]{0:T(128)}, /*index=5*/s32[1]{0:T(128)}, s32[1]{0:T(128)}, s32[1]{0:...) fusion(s32[32]{0:T(128)} %param.10), kind=kLoop, calls=%fused_computation.146 | loop fusion | bytes 152 | tf_op jit(solution)/shard_map/jit(_take)/gather | solution.py:36
  12.5 4.4 %compare_select_fusion.13 = s32[256,1]{0,1:T(1,128)S(1)} fusion(s32[]{:T(128)} %bitcast.25, s32[]{:T(128)} %bitcast.26, s32[]{:T(128)} %bitcast.27, s32[]{:T(128)} %bitcast.28, s32[]{:T(128)} %bitcast.29, s32[]{:T(128)} %bitcast.31, s32[]{:T(128)} %bitcast.30, s32[]{:T(128)S(6)} %mul.71), kind=kLoop, calls=%fused_computation.115 | loop fusion | flops 7936 | bytes 1056 | tf_op jit(solution)/shard_map/jit(_take)/gather | solution.py:36
  16.9 15.7 %select_select_fusion.1 = s32[256]{0:T(256)S(1)} fusion(pred[256]{0:T(512)(128)(4,1)S(1)} %get-tuple-element.47, pred[256]{0:T(512)(128)(4,1)S(1)} %get-tuple-element.48, pred[256]{0:T(512)(128)(4,1)S(1)} %get-tuple-element.49, pred[256]{0:T(512)(128)(4,1)S(1)} %get-tuple-element.50, pred[256]{0:T(512)(128)(4,1)S(1)} %get-tuple-element.51, ...), kind=kLoop, calls=%fused_computation.139 | loop fusion | flops 6400 | bytes 8548 | tf_op jit(solution)/shard_map/jit(_take)/gather | solution.py:36
  32.6 2.0 %gather_fusion.1 = s32[256]{0:T(256)S(1)} fusion(s32[4096]{0:T(1024)} %param.11, s32[1024]{0:T(1024)S(1)} %pad_clamp_fusion), kind=kCustom, calls=%fused_computation.1 | custom fusion | bytes 3072 | tf_op jit(solution)/shard_map/jit(_take)/gather | solution.py:75
  34.6 0.1 compare_reduce_fusion.23
  34.7 0.1 compare_reduce_fusion.22
  34.8 0.1 compare_reduce_fusion.21
  34.8 0.1 compare_reduce_fusion.20
  34.9 0.1 compare_reduce_fusion.19
  34.9 0.1 compare_reduce_fusion.18
  35.0 0.1 compare_reduce_fusion.17
  35.1 0.1 compare_reduce_fusion.16
  35.1 0.1 compare_reduce_fusion.15
  35.2 0.1 compare_reduce_fusion.14
  35.2 0.1 compare_reduce_fusion.13
  35.3 0.1 compare_reduce_fusion.12
  35.3 0.1 compare_reduce_fusion.11
  35.4 0.1 compare_reduce_fusion.10
  35.5 0.1 compare_reduce_fusion.9
  35.5 0.1 compare_reduce_fusion.8
  35.6 0.1 compare_reduce_fusion.7
  35.6 0.1 compare_reduce_fusion.6
  35.7 0.1 compare_reduce_fusion.5
  35.8 0.1 compare_reduce_fusion.4
  35.8 0.1 compare_reduce_fusion.3
  35.9 0.1 compare_reduce_fusion.2
  35.9 0.1 compare_reduce_fusion.1
  36.0 0.1 compare_reduce_fusion
  36.0 4.3 %compare_select_fusion.2 = s32[4096,1]{0,1:T(1,128)S(1)} fusion(s32[]{:T(128)} %bitcast.25, s32[]{:T(128)} %bitcast.26, s32[]{:T(128)} %bitcast.27, s32[]{:T(128)} %bitcast.28, s32[]{:T(128)} %bitcast.29, s32[]{:T(128)} %bitcast.31, s32[]{:T(128)} %bitcast.30), kind=kLoop, calls=%fused_computation.52 | loop fusion | flops 94208 | bytes 16412 | tf_op jit(solution)/shard_map/jit(_take)/gather | solution.py:36
  40.4 15.8 %select_select_fusion = s32[4096]{0:T(1024)S(1)} fusion(pred[4096]{0:T(1024)(128)(4,1)S(1)} %compare_reduce_fusion, pred[4096]{0:T(1024)(128)(4,1)S(1)} %compare_reduce_fusion.1, pred[4096]{0:T(1024)(128)(4,1)S(1)} %compare_reduce_fusion.2, pred[4096]{0:T(1024)(128)(4,1)S(1)} %compare_reduce_fusion.3, pred[4096]{0:T(1024)(128)(4,1)S(1)} %compare_reduce_fusion.4, ...), kind=kLoop, calls=%fused_computation.81 | loop fusion | flops 102400 | bytes 135268 | tf_op jit(solution)/shard_map/jit(_take)/gather | solution.py:36
  56.2 19.3 %gather_fusion = s32[4096]{0:T(1024)S(1)} fusion(s32[4096]{0:T(1024)} %param.11, s32[4096]{0:T(1024)S(1)} %broadcast_clamp_fusion), kind=kCustom, calls=%fused_computation | custom fusion | bytes 49152 | tf_op jit(solution)/shard_map/jit(_take)/gather | solution.py:84
  75.5 1.4 compare_and_fusion
  77.0 0.0 all-gather.2.cloned.1.call-done
  77.0 0.0 copy-done
  77.0 0.0 copy-start.2
  77.0 4.0 %fusion.2 = (f32[4,256]{1,0:T(4,128)S(1)}, f32[4096,256,4]{1,0,2:T(8,128)S(1)}) fusion(pred[256,4096]{0,1:T(8,128)(4,1)S(1)} %compare_and_fusion, bf16[4096,256]{1,0:T(8,128)(2,1)} %all-gather.2.cloned.1.call-done, bf16[256,512]{1,0:T(8,128)(2,1)S(1)} %copy-done), kind=kOutput, calls=%fused_computation.6 | convolution fusion | flops 1086323712 | bytes 19140608 | tf_op jit(solution)/shard_map/rkgd,skd->kgrs/dot_general | solution.py:49
  81.0 0.0 copy-start.1
  81.0 5.7 %copy-done.1 = f32[4096,256,4]{1,0,2:T(8,128)} copy-done((f32[4096,256,4]{1,0,2:T(8,128)}, f32[4096,256,4]{1,0,2:T(8,128)S(1)}, u32[]{:S(2)}) %copy-start.1) | copy-done | bytes 16777240
  86.7 3.6 %fusion = f32[4,256]{1,0:T(4,128)S(1)} fusion(f32[4096,256,4]{1,0,2:T(8,128)S(1)} %get-tuple-element.44, f32[4,256]{1,0:T(4,128)S(1)} %compare_select_fusion.10, pred[256,4096]{0,1:T(8,128)(4,1)S(1)} %compare_and_fusion), kind=kLoop, calls=%fused_computation.4 | loop fusion | flops 16776192 | bytes 17833984 | tf_op jit(solution)/shard_map/reduce_sum | solution.py:57
  90.4 0.0 copy-done.2
  90.4 13.9 %fusion.3 = bf16[256,8192]{1,0:T(8,128)(2,1)} fusion(bf16[4,128,8192]{2,1,0:T(8,128)(2,1)} %bitcast.114, bf16[4096,256]{1,0:T(8,128)(2,1)S(1)} %copy-done.2, f32[4096,256,4]{1,0,2:T(8,128)} %copy-done.1, f32[4,256]{1,0:T(4,128)S(1)} %compare_select_fusion.10, pred[256,4096]{0,1:T(8,128)(4,1)S(1)} %compare_and_fusion, f32[4,256]{1,0:T(4,128)S(1)} %get-tuple-element.10, ...), kind=kOutput, calls=%fused_computation.8 | convolution fusion | flops 3240493056 | bytes 31469568 | tf_op jit(solution)/shard_map/kgrd,kgdm->rm/dot_general | solution.py:91
  104.3 2.6 %copy.22 = bf16[32,16,8,512]{3,2,0,1:T(8,128)(2,1)S(1)} copy(bf16[32,16,8,512]{3,2,1,0:T(8,128)(2,1)} %bitcast.107) | data formatting | bytes 8388608 | tf_op jit(solution)/shard_map/reshape | solution.py:23
  106.9 57.7 %all_to_all.5 = bf16[16,256,512]{2,1,0:T(8,128)(2,1)} all-to-all(bf16[16,256,512]{2,1,0:T(8,128)(2,1)S(1)} %bitcast.106), channel_id=1, replica_groups=mesh['ctx'=16,'grp'=16] {'grp'}, dimensions={0} | all-to-all | bytes 8388608 | tf_op jit(solution)/shard_map/all_to_all | solution.py:29
  164.6 3.5 %reduce_sum.22 = bf16[256,512]{1,0:T(8,128)(2,1)} reduce(bf16[16,256,512]{2,1,0:T(8,128)(2,1)} %all_to_all.5, bf16[]{:T(256)} %constant.148.clone.1), dimensions={0}, to_apply=%region_2.3 | reduce | flops 1966080 | bytes 4456450 | tf_op jit(solution)/shard_map/reduce_sum | solution.py:30
  (22 shorter events, 0.6 us)
Async XLA Ops:
  6.5 70.5 %copy-start = (bf16[256,512]{1,0:T(8,128)(2,1)S(1)}, bf16[256,512]{1,0:T(8,128)(2,1)}, u32[]{:S(2)}) copy-start(bf16[256,512]{1,0:T(8,128)(2,1)} %param.6) | copy-start | bytes 786436
  6.5 70.5 %all-gather.2.cloned.1.call-start = ((), (), s32[]{:S(2)}) async-start(), calls=%async_computation.1 | async-start | bytes 2228224 | tf_op jit(solution)/shard_map/all_gather | solution.py:18
  77.0 13.4 %copy-start.2 = (bf16[4096,256]{1,0:T(8,128)(2,1)S(1)}, bf16[4096,256]{1,0:T(8,128)(2,1)}, u32[]{:S(2)}) copy-start(bf16[4096,256]{1,0:T(8,128)(2,1)} %all-gather.2.cloned.1.call-done) | copy-start | bytes 6291460
  81.0 5.7 %copy-start.1 = (f32[4096,256,4]{1,0,2:T(8,128)}, f32[4096,256,4]{1,0,2:T(8,128)S(1)}, u32[]{:S(2)}) copy-start(f32[4096,256,4]{1,0,2:T(8,128)S(1)} %get-tuple-element.44) | copy-start | bytes 50331652
Sparse Core Ops, SparseCore 0:
  9.2 40.6 all-gather.1
where the time goes:
time: 176 us; the launch traced here: 175 us
  blocking collectives  57.7 us (33%)
  other arithmetic  51.4 us (29%)
  local copies, waits for them, and re-layouts  34.4 us (20%)
  matrix products  17.9 us (10%)
  between operations  13.6 us (8%)
    all_to_all x1, blocking collectives, summed_on_arrival(): lax.all_to_all(parts, axis, split_axis=0, concat_axis=0, tiled=True)  57.7 us
    gather x42, other arithmetic, span_positions(): return jnp.take(span_order, rows // span_len) * span_len + rows % span_len  42 us
    gather x1, local copies, waits for them, and re-layouts, shards(): key_doc = jnp.take(document, key_pos)  19.3 us
    dot_general x1, matrix products, shards(): jnp.einsum('kgrd,kgdm->rm', attended, weight_view, preferred_element_type...  13.9 us
    unnamed x6, local copies, waits for them, and re-layouts  5.7 us
    dot_general x1, matrix products, attend(): jnp.einsum('rkgd,skd->kgrs', grouped, key_view, preferred_element_type=jn...  4 us
    gather x2, local copies, waits for them, and re-layouts, span_positions(): return jnp.take(span_order, rows // span_len) * span_len + rows % span_len  3.91 us
    reduce_sum x1, other arithmetic, attend(): new_sum = run_sum * rescale + jnp.sum(probs, axis=-1)  3.61 us
  transfers between devices with their start and end apart: 1, of which 0 were waited for; matrix products, arithmetic and copies ran while one was open for 39% of the time, Pallas kernels for 0%

commit v1 on v0

v1 whole, which is shorter than its diff:
```python
import math

import jax
import jax.numpy as jnp
from jax import lax
from jax.experimental import pallas as pl
from jax.experimental.pallas import tpu as pltpu
from jax.sharding import PartitionSpec as P


HEAD_DIM = 128
QUERY_GROUP = 8
SPAN = 128
CHUNK = 256
NEG = -1e30
NZ, NX, NY = 8, 4, 4
FETCHES = 8

VMEM = pl.BlockSpec(memory_space=pltpu.VMEM)
SMEM = pl.BlockSpec(memory_space=pltpu.SMEM)
HBM = pl.BlockSpec(memory_space=pltpu.HBM)
BOTH = ("ctx", "grp")
STEPS = (2, 1, 3)

OTHER_CORE = [(i, i ^ 1) for i in range(2 * NZ)]
FAR_SIDE = [(z * 2 + c, (z + 4) % NZ * 2 + c) for z in range(NZ) for c in range(2)]


def ring(k):
    return [(z * 2 + c, (z + k * (1 - 2 * c)) % NZ * 2 + c) for z in range(NZ) for c in range(2)]


def plane_steps(k, x_core):
    pairs = []
    for ctx in range(2 * NZ):
        for x in range(NX):
            for y in range(NY):
                to = ((x + k) % NX, y) if ctx % 2 == x_core else (x, (y + k) % NY)
                pairs.append(((ctx * NX + x) * NY + y, (ctx * NX + to[0]) * NY + to[1]))
    return pairs


CAME = [(0, 0, 1), (0, 1, 1), (4, 0, 1), (4, 1, 1)]
CAME += [(-k, 0, 2) for k in (1, 2, 3)] + [(k, 1, 2) for k in (1, 2, 3)]


def gathered(own):
    other = lax.ppermute(own, "ctx", OTHER_CORE)
    chip = jnp.concatenate([own, other], axis=0)
    two = lax.ppermute(chip, "ctx", ring(2))
    one = lax.ppermute(chip, "ctx", ring(1))
    far = lax.ppermute(own, "ctx", FAR_SIDE)
    three = lax.ppermute(two, "ctx", ring(1))
    passed = [lax.ppermute(x, "ctx", OTHER_CORE) for x in (one, two, three)]
    return [own, other, far, lax.ppermute(far, "ctx", OTHER_CORE), one, two, three] + passed


def block_of(where, k, j):
    core, ex, why = where[0] % 2, where[1], where[2]
    by_x = (ex + k) % NX * NY + (why + j) % NY
    by_y = (ex + j) % NX * NY + (why + k) % NY
    return jnp.where(core == 0, by_x, by_y)


def project(where, att, w_ref, outs):
    cols = w_ref.shape[1] // (NX * NY)
    for k in STEPS + (0,):
        for j in range(4):
            at = pl.multiple_of(block_of(where, k, j) * cols, cols)
            part = jnp.dot(att, w_ref[:, pl.ds(at, cols)], preferred_element_type=jnp.float32)
            outs[k][j] = part.astype(jnp.bfloat16)


def fetch_kernel(where, w_hbm, w_ref, sems):
    rows = w_ref.shape[0] // FETCHES
    copies = [
        pltpu.make_async_copy(
            w_hbm.at[i * rows : (i + 1) * rows], w_ref.at[i * rows : (i + 1) * rows], sems.at[i]
        )
        for i in range(FETCHES)
    ]
    for copy in copies:
        copy.start()
    for copy in copies:
        copy.wait()


def fetched(where, weight):
    return pl.pallas_call(
        fetch_kernel,
        out_shape=jax.ShapeDtypeStruct(weight.shape, weight.dtype),
        in_specs=[SMEM, HBM],
        out_specs=VMEM,
        scratch_shapes=[pltpu.SemaphoreType.DMA((FETCHES,))],
        compiler_params=pltpu.CompilerParams(vmem_limit_bytes=40 << 20),
        cost_estimate=pl.CostEstimate(flops=0, bytes_accessed=16 << 20, transcendentals=0),
        name="fetch",
    )(where, weight)


def place(where, kv_refs, keys, values):
    zed, core = where[0] // 2, where[0] % 2
    for (steps, first, parts), kv in zip(CAME, kv_refs):
        plane = (zed + (steps if parts == 1 else steps * (1 - 2 * core)) + NZ) % NZ * 2
        for part in range(parts):
            source = plane + (core + first + part) % 2
            for half in range(2):
                at = pl.multiple_of(where[6 + source * 2 + half] * SPAN, SPAN)
                rows = slice((part * 2 + half) * SPAN, (part * 2 + half + 1) * SPAN)
                keys[pl.ds(at, SPAN), :] = kv[rows, :HEAD_DIM]
                values[pl.ds(at, SPAN), :] = kv[rows, HEAD_DIM:]


def attended(where, slot, q_ref, keys, values, acc):
    heads = q_ref.shape[1] // HEAD_DIM
    lanes = heads * SPAN
    scale = math.log2(math.e) / math.sqrt(HEAD_DIM)
    queries = jnp.concatenate(
        [q_ref[:, h * HEAD_DIM : (h + 1) * HEAD_DIM] for h in range(heads)], axis=0
    )
    at = where[6 + slot] * SPAN
    pos = at + lax.broadcasted_iota(jnp.int32, (1, lanes), 1) % SPAN
    low, low0 = jnp.zeros_like(pos), jnp.int32(0)
    for start in [where[i] for i in (3, 4, 5)]:
        low = jnp.where(start <= pos, start, low)
        low0 = jnp.where(start <= at, start, low0)
    acc[...] = jnp.zeros_like(acc)
    kv_iota = lax.broadcasted_iota(jnp.int32, (CHUNK, lanes), 0)

    def step(chunk, carry):
        top, total = carry
        rows = pl.ds(pl.multiple_of(chunk * CHUNK, CHUNK), CHUNK)
        scores = lax.dot_general(
            keys[rows, :], queries, (((1,), (1,)), ((), ())), preferred_element_type=jnp.float32
        )
        kv_pos = kv_iota + chunk * CHUNK
        visible = (kv_pos >= low) & (kv_pos <= pos)
        scores = jnp.where(visible, scores * scale, NEG)
        higher = jnp.maximum(top, jnp.max(scores, axis=0, keepdims=True))
        rescale = jnp.exp2(top - higher)
        probs = jnp.exp2(scores - higher)
        total = total * rescale + jnp.sum(probs, axis=0, keepdims=True)
        mixed = lax.dot_general(
            values[rows, :], probs.astype(jnp.bfloat16), (((0,), (0,)), ((), ())),
            preferred_element_type=jnp.float32,
        )
        acc[...] = acc[...] * rescale + mixed
        return higher, total

    start = (jnp.full((1, lanes), NEG, jnp.float32), jnp.zeros((1, lanes), jnp.float32))
    _, total = lax.fori_loop(low0 // CHUNK, (at + SPAN - 1) // CHUNK + 1, step, start)
    mixed = acc[...] / total
    return jnp.concatenate(
        [mixed[:, h * SPAN : (h + 1) * SPAN].T.astype(jnp.bfloat16) for h in range(heads)], axis=1
    )


def theirs_kernel(where, q_ref, w_ref, *refs):
    kv_refs, (keys, values), outs, acc = refs[:-7], refs[-7:-5], refs[-5:-1], refs[-1]
    place(where, kv_refs, keys, values)
    ctx = where[0]
    slot = (ctx // 2 * 2 + 1 - ctx % 2) * 2 + ctx % 2
    project(where, attended(where, slot, q_ref, keys, values, acc), w_ref, outs)


def mine_kernel(where, q_ref, w_ref, keys, values, *refs):
    outs, acc = refs[:4], refs[4]
    slot = where[0] * 2 + where[0] % 2
    project(where, attended(where, slot, q_ref, keys, values, acc), w_ref, outs)


def attend(kernel, where, queries, weight, kv, seq, keep):
    width = queries.shape[1]
    cols = weight.shape[1] // (NX * NY)
    kept = [jax.ShapeDtypeStruct((seq, HEAD_DIM), jnp.bfloat16)] * (2 * keep)
    parts = [jax.ShapeDtypeStruct((4, SPAN, cols), jnp.bfloat16)] * 4
    return pl.pallas_call(
        kernel,
        out_shape=kept + parts,
        in_specs=[SMEM] + [VMEM] * (2 + len(kv)),
        out_specs=[VMEM] * (len(kept) + 4),
        scratch_shapes=[pltpu.VMEM((HEAD_DIM, width), jnp.float32)],
        compiler_params=pltpu.CompilerParams(vmem_limit_bytes=24 << 20),
        cost_estimate=pl.CostEstimate(
            flops=2 << 30, bytes_accessed=12 << 20, transcendentals=2 << 20
        ),
    )(where, queries, weight, *kv)


def total_of(parts):
    return sum(p.astype(jnp.float32) for p in parts).astype(jnp.bfloat16)


def reduced(parts):
    got = [parts[0]]
    got += [lax.ppermute(parts[k], BOTH, plane_steps(k, 0)) for k in STEPS]
    line = [total_of([g[j] for g in got]) for j in range(4)]
    last = [lax.ppermute(line[j], BOTH, plane_steps(j, 1)) for j in STEPS]
    return total_of([line[0]] + last)


def shards(queries, keys, values, out_weight, span_order, document):
    ctx, grp = lax.axis_index("ctx"), lax.axis_index("grp")
    core = ctx % 2
    local_heads = queries.shape[1] // HEAD_DIM
    at = grp * local_heads // QUERY_GROUP * HEAD_DIM
    own = jnp.concatenate(
        [lax.dynamic_slice_in_dim(a, at, HEAD_DIM, 1) for a in (keys, values)], axis=1
    )
    kept = lax.dynamic_slice_in_dim(queries, core * SPAN, SPAN, 0)
    away = lax.dynamic_slice_in_dim(queries, (1 - core) * SPAN, SPAN, 0)
    swapped = lax.ppermute(away, "ctx", OTHER_CORE)
    starts = jnp.sum(document[None, :] < jnp.arange(1, 4)[:, None], axis=1, dtype=jnp.int32)
    index = jnp.stack([ctx, grp // NY, grp % NY]).astype(jnp.int32)
    where = jnp.concatenate([index, starts, span_order])
    weight = fetched(where, out_weight)
    blocks = gathered(own)
    seq = document.shape[0]
    *kv, b0, b1, b2, b3 = attend(theirs_kernel, where, swapped, weight, blocks, seq, True)
    parts = attend(mine_kernel, where, kept, weight, kv, seq, False)
    back = lax.ppermute(reduced([b0, b1, b2, b3]), "ctx", OTHER_CORE)
    mine = reduced(parts)
    return jnp.concatenate(
        [jnp.where(core == 0, mine, back), jnp.where(core == 0, back, mine)], axis=0
    )


def solution(mesh):
    in_specs = (P("ctx", "grp"), P("ctx", None), P("ctx", None), P("grp", None), P(), P())
    out_specs = P("ctx", "grp")
    return jax.shard_map(shards, mesh=mesh, in_specs=in_specs, out_specs=out_specs, check_vma=False)
```

time: 176 us -> 82.9 us (0.47)
  the two profiles are of different devices: /device:TPU:96 before, /device:TPU:2 now
where the time goes in v1:
time: 82.9 us; the launch traced here: 82.7 us
  starting transfers between devices  33.8 us (41%)
  waiting for transfers between devices  32.3 us (39%)
  Pallas kernels  11.4 us (14%)
  local copies, waits for them, and re-layouts  2.6 us (3%)
  other arithmetic  2.39 us (3%)
    ppermute x6, waiting for transfers between devices, reduced(): got += [lax.ppermute(parts[k], BOTH, plane_steps(k, 0)) for k in STEPS]  12.7 us
    ppermute x6, starting transfers between devices, reduced(): last = [lax.ppermute(line[j], BOTH, plane_steps(j, 1)) for j in STEPS]  11.4 us
    ppermute x6, starting transfers between devices, reduced(): got += [lax.ppermute(parts[k], BOTH, plane_steps(k, 0)) for k in STEPS]  8.62 us
    pallas_call x2, Pallas kernels, attend(): pl.pallas_call(kernel, out_shape=kept + parts, in_specs=[SMEM] + [VMEM] *...  7.34 us
    ppermute x1, waiting for transfers between devices, gathered(): two = lax.ppermute(chip, 'ctx', ring(2))  6.06 us
    ppermute x6, waiting for transfers between devices, reduced(): last = [lax.ppermute(line[j], BOTH, plane_steps(j, 1)) for j in STEPS]  4.98 us
    ppermute x1, waiting for transfers between devices, gathered(): far = lax.ppermute(own, 'ctx', FAR_SIDE)  4.44 us
    pallas_call x1, Pallas kernels, fetched(): pl.pallas_call(fetch_kernel, out_shape=jax.ShapeDtypeStruct(weight.shape,...  4.02 us
  transfers between devices with their start and end apart: 23, of which 10 were waited for; matrix products, arithmetic and copies ran while one was open for 4% of the time, Pallas kernels for 8%

profile of v1, /device:TPU:2, one launch (start us, length us, event | category | flops | bytes accessed | tf_op | source)
XLA Modules:
  0.0 82.7 jit_solution(12329290039740862054)
XLA Ops:
  0.0 0.9 %constant_dynamic-slice_fusion = (bf16[256,128]{1,0:T(8,128)(2,1)S(1)}, bf16[256,128]{1,0:T(8,128)(2,1)S(1)}) fusion(bf16[256,1024]{1,0:T(8,128)(2,1)} %param.8, s32[]{:T(128)S(6)} %select_n.47, bf16[256,1024]{1,0:T(8,128)(2,1)} %param.7), kind=kLoop, calls=%fused_computation.30 | loop fusion | bytes 262148 | tf_op jit(solution)/shard_map/dynamic_slice | solution.py:208
  0.9 0.1 collective-permute-start.1
  1.0 1.3 %collective-permute-done.1.refs_1_ = bf16[256,256]{1,0:T(8,128)(2,1)S(1)} collective-permute-done((bf16[256,256]{1,0:T(8,128)(2,1)S(1)}, bf16[256,256]{1,0:T(8,128)(2,1)S(1)}, u32[]{:S(2)}, u32[]{:S(2)}) %collective-permute-start.1) | collective-permute-done | bytes 131104 | tf_op jit(solution)/shard_map/ppermute | solution.py:48
  2.4 3.3 %collective-permute-start.5 = (bf16[512,256]{1,0:T(8,128)(2,1)S(1)}, bf16[512,256]{1,0:T(8,128)(2,1)S(1)}, u32[]{:S(2)}, u32[]{:S(2)}) collective-permute-start(bf16[512,256]{1,0:T(8,128)(2,1)S(1)} %pad_maximum_fusion), channel_id=1, source_target_pairs={{0,64},{16,208},{32,96},{48,240},{64,128},{80,16},{96,160},{112,48... | collective-permute-start | bytes 786440 | tf_op jit(solution)/shard_map/ppermute | solution.py:50
  5.7 1.9 %collective-permute-start.4 = (bf16[512,256]{1,0:T(8,128)(2,1)S(1)}, bf16[512,256]{1,0:T(8,128)(2,1)S(1)}, u32[]{:S(2)}, u32[]{:S(2)}) collective-permute-start(bf16[512,256]{1,0:T(8,128)(2,1)S(1)} %pad_maximum_fusion), channel_id=1, source_target_pairs={{0,32},{16,240},{32,64},{48,16},{64,96},{80,48},{96,128},{112,80},... | collective-permute-start | bytes 786440 | tf_op jit(solution)/shard_map/ppermute | solution.py:51
  7.6 6.1 %collective-permute-done.5.refs_5_ = bf16[512,256]{1,0:T(8,128)(2,1)S(1)} collective-permute-done((bf16[512,256]{1,0:T(8,128)(2,1)S(1)}, bf16[512,256]{1,0:T(8,128)(2,1)S(1)}, u32[]{:S(2)}, u32[]{:S(2)}) %collective-permute-start.5) | collective-permute-done | bytes 262176 | tf_op jit(solution)/shard_map/ppermute | solution.py:50
  13.7 3.3 %collective-permute-start.6 = (bf16[512,256]{1,0:T(8,128)(2,1)S(1)}, bf16[512,256]{1,0:T(8,128)(2,1)S(1)}, u32[]{:S(2)}, u32[]{:S(2)}) collective-permute-start(bf16[512,256]{1,0:T(8,128)(2,1)S(1)} %collective-permute-done.5.refs_5_), channel_id=1, source_target_pairs={{0,32},{16,240},{32,64},{48,16},{64,96},{80,48},{96,128},{112,80},... | collective-permute-start | bytes 786440 | tf_op jit(solution)/shard_map/ppermute | solution.py:53
  17.0 3.9 %collective-permute-start.2 = (bf16[256,256]{1,0:T(8,128)(2,1)S(1)}, bf16[256,256]{1,0:T(8,128)(2,1)S(1)}, u32[]{:S(2)}, u32[]{:S(2)}) collective-permute-start(bf16[256,256]{1,0:T(8,128)(2,1)S(1)} %pad_maximum_fusion.2.refs_0_), channel_id=1, source_target_pairs={{0,128},{16,144},{32,160},{48,176},{64,192},{80,208},{96,224},{112... | collective-permute-start | bytes 393224 | tf_op jit(solution)/shard_map/ppermute | solution.py:52
  20.9 0.0 collective-permute-start.8
  20.9 0.0 collective-permute-done.4.refs_4_
  20.9 0.5 collective-permute-start.7
  21.5 2.8 %collective-permute-done.6.refs_6_ = bf16[512,256]{1,0:T(8,128)(2,1)S(1)} collective-permute-done((bf16[512,256]{1,0:T(8,128)(2,1)S(1)}, bf16[512,256]{1,0:T(8,128)(2,1)S(1)}, u32[]{:S(2)}, u32[]{:S(2)}) %collective-permute-start.6) | collective-permute-done | bytes 262176 | tf_op jit(solution)/shard_map/ppermute | solution.py:53
  24.3 0.0 collective-permute-start.9
  24.3 1.0 %constant_dynamic-slice_fusion.3 = (bf16[128,512]{1,0:T(8,128)(2,1)S(1)}, bf16[128,512]{1,0:T(8,128)(2,1)S(1)}) fusion(bf16[256,512]{1,0:T(8,128)(2,1)} %param.6, s32[]{:T(128)S(6)} %select_n.44, s32[]{:T(128)S(6)} %select_n.45), kind=kLoop, calls=%fused_computation.33 | loop fusion | bytes 524296 | tf_op jit(solution)/shard_map/dynamic_slice | solution.py:210
  25.3 0.6 collective-permute-start
  25.9 4.4 %collective-permute-done.2.refs_2_ = bf16[256,256]{1,0:T(8,128)(2,1)S(1)} collective-permute-done((bf16[256,256]{1,0:T(8,128)(2,1)S(1)}, bf16[256,256]{1,0:T(8,128)(2,1)S(1)}, u32[]{:S(2)}, u32[]{:S(2)}) %collective-permute-start.2) | collective-permute-done | bytes 131104 | tf_op jit(solution)/shard_map/ppermute | solution.py:52
  30.3 0.0 collective-permute-start.3
  30.3 0.9 %convert_reduce_fusion = s32[3]{0:T(128)S(1)} fusion(s32[4096]{0:T(1024)} %param.11, s32[3]{0:T(128)S(1)} %iota_add_fusion), kind=kLoop, calls=%fused_computation.29 | loop fusion | flops 36861 | bytes 16408 | tf_op jit(solution)/shard_map/reduce_sum | solution.py:213
  31.3 0.7 concatenate.12.where
  32.0 4.0 %fetch.1.w_ref = bf16[512,8192]{1,0:T(8,128)(2,1)S(1)} custom-call(s32[38]{0:T(128)S(1)} %concatenate.12.where, bf16[512,8192]{1,0:T(8,128)(2,1)} %w_hbm.1), custom_call_target="tpu_custom_call" | custom-call | bytes 16777216 | tf_op jit(solution)/shard_map/fetch/pallas_call | solution.py:89
  36.0 0.0 collective-permute-done.q_ref
  36.0 0.0 collective-permute-done.3.refs_3_
  36.0 0.0 collective-permute-done.8.refs_8_
  36.0 0.0 collective-permute-done.7.refs_7_
  36.1 0.0 collective-permute-done.9.refs_9_
  36.1 4.4 %shard_map.64 = (bf16[4096,128]{1,0:T(8,128)(2,1)S(1)}, bf16[4096,128]{1,0:T(8,128)(2,1)S(1)}, bf16[4,128,512]{2,1,0:T(8,128)(2,1)S(1)}, bf16[4,128,512]{2,1,0:T...) custom-call(s32[38]{0:T(128)S(1)} %concatenate.12.where, ...), custom_call_target="tpu_custom_call" | custom-call | flops 2147483648 | bytes 12582912 | tf_op jit(solution)/shard_map/pallas_call | solution.py:177
  40.5 2.2 %collective-permute-start.16 = (bf16[4,128,512]{2,1,0:T(8,128)(2,1)S(1)}, bf16[4,128,512]{2,1,0:T(8,128)(2,1)S(1)}, u32[]{:S(2)}, u32[]{:S(2)}) collective-permute-start(bf16[4,128,512]{2,1,0:T(8,128)(2,1)S(1)} %get-tuple-element.22), channel_id=1, source_target_pairs={{0,8},{1,9},{2,10},{3,11},{4,12},{5,13},{6,14},{7,15},{8,0},{9,1},... | collective-permute-start | bytes 1572872 | tf_op jit(solution)/shard_map/ppermute | solution.py:196
  42.7 0.0 collective-permute-start.17
  42.7 2.0 %collective-permute-start.18 = (bf16[4,128,512]{2,1,0:T(8,128)(2,1)S(1)}, bf16[4,128,512]{2,1,0:T(8,128)(2,1)S(1)}, u32[]{:S(2)}, u32[]{:S(2)}) collective-permute-start(bf16[4,128,512]{2,1,0:T(8,128)(2,1)S(1)} %get-tuple-element.24), channel_id=1, source_target_pairs={{0,12},{1,13},{2,14},{3,15},{4,0},{5,1},{6,2},{7,3},{8,4},{9,5},{1... | collective-permute-start | bytes 1572872 | tf_op jit(solution)/shard_map/ppermute | solution.py:196
  44.7 2.9 %shard_map.65 = (bf16[4,128,512]{2,1,0:T(8,128)(2,1)S(1)}, bf16[4,128,512]{2,1,0:T(8,128)(2,1)S(1)}, bf16[4,128,512]{2,1,0:T(8,128)(2,1)S(1)}, bf16[4,128,512]{2,1,0:T(8,128)(2,1)S(1)}) custom-call(s32[38]{0:T(128)S(1)} %concatenate.12.where, bf16[128,512]{1,0:T(8,128)(2,1)S(1)} %get-tuple-element.33.q_ref, bf16[512,8192]{1,0:T(8,128)(2,1)S(1)} %fetch.1.w_ref, ...), custom_call_target="tpu_custom_call" | custom-call | flops 2147483648 | bytes 12582912 | tf_op jit(solution)/shard_map/pallas_call | solution.py:177
  47.7 1.8 %collective-permute-start.10 = (bf16[4,128,512]{2,1,0:T(8,128)(2,1)S(1)}, bf16[4,128,512]{2,1,0:T(8,128)(2,1)S(1)}, u32[]{:S(2)}, u32[]{:S(2)}) collective-permute-start(bf16[4,128,512]{2,1,0:T(8,128)(2,1)S(1)} %get-tuple-element.18), channel_id=1, source_target_pairs={{0,8},{1,9},{2,10},{3,11},{4,12},{5,13},{6,14},{7,15},{8,0},{9,1},... | collective-permute-start | bytes 1572872 | tf_op jit(solution)/shard_map/ppermute | solution.py:196
  49.4 2.6 %collective-permute-start.11 = (bf16[4,128,512]{2,1,0:T(8,128)(2,1)S(1)}, bf16[4,128,512]{2,1,0:T(8,128)(2,1)S(1)}, u32[]{:S(2)}, u32[]{:S(2)}) collective-permute-start(bf16[4,128,512]{2,1,0:T(8,128)(2,1)S(1)} %get-tuple-element.19), channel_id=1, source_target_pairs={{0,4},{1,5},{2,6},{3,7},{4,8},{5,9},{6,10},{7,11},{8,12},{9,13},{1... | collective-permute-start | bytes 1572872 | tf_op jit(solution)/shard_map/ppermute | solution.py:196
  52.0 0.0 collective-permute-done.16
  52.0 0.0 collective-permute-start.12
  52.0 4.9 %collective-permute-done.17 = bf16[4,128,512]{2,1,0:T(8,128)(2,1)S(1)} collective-permute-done((bf16[4,128,512]{2,1,0:T(8,128)(2,1)S(1)}, bf16[4,128,512]{2,1,0:T(8,128)(2,1)S(1)}, u32[]{:S(2)}, u32[]{:S(2)}) %collective-permute-start.17) | collective-permute-done | bytes 524320 | tf_op jit(solution)/shard_map/ppermute | solution.py:196
  57.0 0.0 collective-permute-done.18
  57.0 0.2 fusion.11
  57.2 3.3 %collective-permute-start.19 = (bf16[128,512]{1,0:T(8,128)(2,1)S(1)}, bf16[128,512]{1,0:T(8,128)(2,1)S(1)}, u32[]{:S(2)}, u32[]{:S(2)}) collective-permute-start(bf16[128,512]{1,0:T(8,128)(2,1)S(1)} %get-tuple-element.30), channel_id=1, source_target_pairs={{0,2},{1,3},{2,0},{3,1},{4,6},{5,7},{6,4},{7,5},{8,10},{9,11},{10,... | collective-permute-start | bytes 393224 | tf_op jit(solution)/shard_map/ppermute | solution.py:198
  60.4 1.1 %collective-permute-start.21 = (bf16[128,512]{1,0:T(8,128)(2,1)S(1)}, bf16[128,512]{1,0:T(8,128)(2,1)S(1)}, u32[]{:S(2)}, u32[]{:S(2)}) collective-permute-start(bf16[128,512]{1,0:T(8,128)(2,1)S(1)} %get-tuple-element.31), channel_id=1, source_target_pairs={{0,3},{1,0},{2,1},{3,2},{4,7},{5,4},{6,5},{7,6},{8,11},{9,8},{10,9... | collective-permute-start | bytes 393224 | tf_op jit(solution)/shard_map/ppermute | solution.py:198
  61.5 2.9 %collective-permute-done.10 = bf16[4,128,512]{2,1,0:T(8,128)(2,1)S(1)} collective-permute-done((bf16[4,128,512]{2,1,0:T(8,128)(2,1)S(1)}, bf16[4,128,512]{2,1,0:T(8,128)(2,1)S(1)}, u32[]{:S(2)}, u32[]{:S(2)}) %collective-permute-start.10) | collective-permute-done | bytes 524320 | tf_op jit(solution)/shard_map/ppermute | solution.py:196
  64.4 1.8 %collective-permute-start.20 = (bf16[128,512]{1,0:T(8,128)(2,1)S(1)}, bf16[128,512]{1,0:T(8,128)(2,1)S(1)}, u32[]{:S(2)}, u32[]{:S(2)}) collective-permute-start(bf16[128,512]{1,0:T(8,128)(2,1)S(1)} %get-tuple-element.32), channel_id=1, source_target_pairs={{0,1},{1,2},{2,3},{3,0},{4,5},{5,6},{6,7},{7,4},{8,9},{9,10},{10,1... | collective-permute-start | bytes 393224 | tf_op jit(solution)/shard_map/ppermute | solution.py:198
  66.2 4.9 %collective-permute-done.11 = bf16[4,128,512]{2,1,0:T(8,128)(2,1)S(1)} collective-permute-done((bf16[4,128,512]{2,1,0:T(8,128)(2,1)S(1)}, bf16[4,128,512]{2,1,0:T(8,128)(2,1)S(1)}, u32[]{:S(2)}, u32[]{:S(2)}) %collective-permute-start.11) | collective-permute-done | bytes 524320 | tf_op jit(solution)/shard_map/ppermute | solution.py:196
  71.0 0.0 collective-permute-done.12
  71.0 0.2 fusion.7
  71.2 3.3 %collective-permute-start.13 = (bf16[128,512]{1,0:T(8,128)(2,1)S(1)}, bf16[128,512]{1,0:T(8,128)(2,1)S(1)}, u32[]{:S(2)}, u32[]{:S(2)}) collective-permute-start(bf16[128,512]{1,0:T(8,128)(2,1)S(1)} %get-tuple-element.27), channel_id=1, source_target_pairs={{0,2},{1,3},{2,0},{3,1},{4,6},{5,7},{6,4},{7,5},{8,10},{9,11},{10,... | collective-permute-start | bytes 393224 | tf_op jit(solution)/shard_map/ppermute | solution.py:198
  74.5 1.1 %collective-permute-start.15 = (bf16[128,512]{1,0:T(8,128)(2,1)S(1)}, bf16[128,512]{1,0:T(8,128)(2,1)S(1)}, u32[]{:S(2)}, u32[]{:S(2)}) collective-permute-start(bf16[128,512]{1,0:T(8,128)(2,1)S(1)} %get-tuple-element.28), channel_id=1, source_target_pairs={{0,3},{1,0},{2,1},{3,2},{4,7},{5,4},{6,5},{7,6},{8,11},{9,8},{10,9... | collective-permute-start | bytes 393224 | tf_op jit(solution)/shard_map/ppermute | solution.py:198
  75.6 0.0 collective-permute-done.19
  75.6 1.0 %collective-permute-start.14 = (bf16[128,512]{1,0:T(8,128)(2,1)S(1)}, bf16[128,512]{1,0:T(8,128)(2,1)S(1)}, u32[]{:S(2)}, u32[]{:S(2)}) collective-permute-start(bf16[128,512]{1,0:T(8,128)(2,1)S(1)} %get-tuple-element.29), channel_id=1, source_target_pairs={{0,1},{1,2},{2,3},{3,0},{4,5},{5,6},{6,7},{7,4},{8,9},{9,10},{10,1... | collective-permute-start | bytes 393224 | tf_op jit(solution)/shard_map/ppermute | solution.py:198
  76.6 0.0 collective-permute-done.21
  76.6 0.0 collective-permute-done.20
  76.6 0.1 fusion.2
  76.7 0.1 collective-permute-start.22
  76.8 1.0 %collective-permute-done.13 = bf16[128,512]{1,0:T(8,128)(2,1)S(1)} collective-permute-done((bf16[128,512]{1,0:T(8,128)(2,1)S(1)}, bf16[128,512]{1,0:T(8,128)(2,1)S(1)}, u32[]{:S(2)}, u32[]{:S(2)}) %collective-permute-start.13) | collective-permute-done | bytes 131104 | tf_op jit(solution)/shard_map/ppermute | solution.py:198
  77.8 1.7 %collective-permute-done.15 = bf16[128,512]{1,0:T(8,128)(2,1)S(1)} collective-permute-done((bf16[128,512]{1,0:T(8,128)(2,1)S(1)}, bf16[128,512]{1,0:T(8,128)(2,1)S(1)}, u32[]{:S(2)}, u32[]{:S(2)}) %collective-permute-start.15) | collective-permute-done | bytes 131104 | tf_op jit(solution)/shard_map/ppermute | solution.py:198
  79.6 2.2 %collective-permute-done.14 = bf16[128,512]{1,0:T(8,128)(2,1)S(1)} collective-permute-done((bf16[128,512]{1,0:T(8,128)(2,1)S(1)}, bf16[128,512]{1,0:T(8,128)(2,1)S(1)}, u32[]{:S(2)}, u32[]{:S(2)}) %collective-permute-start.14) | collective-permute-done | bytes 131104 | tf_op jit(solution)/shard_map/ppermute | solution.py:198
  81.8 0.0 collective-permute-done.22
  81.8 0.1 broadcast_select_fusion.1
  81.9 0.7 pad_maximum_fusion.1
  (4 shorter events, 0.1 us)
Async XLA Ops:
  0.9 1.4 %collective-permute-start.1 = (bf16[256,256]{1,0:T(8,128)(2,1)S(1)}, bf16[256,256]{1,0:T(8,128)(2,1)S(1)}, u32[]{:S(2)}, u32[]{:S(2)}) collective-permute-start(bf16[256,256]{1,0:T(8,128)(2,1)S(1)} %pad_maximum_fusion.2.refs_0_), channel_id=1, source_target_pairs={{0,16},{16,0},{32,48},{48,32},{64,80},{80,64},{96,112},{112,96},{1... | collective-permute-start | bytes 393224 | tf_op jit(solution)/shard_map/ppermute | solution.py:48
  2.4 11.3 %collective-permute-start.5 = (bf16[512,256]{1,0:T(8,128)(2,1)S(1)}, bf16[512,256]{1,0:T(8,128)(2,1)S(1)}, u32[]{:S(2)}, u32[]{:S(2)}) collective-permute-start(bf16[512,256]{1,0:T(8,128)(2,1)S(1)} %pad_maximum_fusion), channel_id=1, source_target_pairs={{0,64},{16,208},{32,96},{48,240},{64,128},{80,16},{96,160},{112,48... | collective-permute-start | bytes 786440 | tf_op jit(solution)/shard_map/ppermute | solution.py:50
  5.7 15.2 %collective-permute-start.4 = (bf16[512,256]{1,0:T(8,128)(2,1)S(1)}, bf16[512,256]{1,0:T(8,128)(2,1)S(1)}, u32[]{:S(2)}, u32[]{:S(2)}) collective-permute-start(bf16[512,256]{1,0:T(8,128)(2,1)S(1)} %pad_maximum_fusion), channel_id=1, source_target_pairs={{0,32},{16,240},{32,64},{48,16},{64,96},{80,48},{96,128},{112,80},... | collective-permute-start | bytes 786440 | tf_op jit(solution)/shard_map/ppermute | solution.py:51
  13.7 10.6 %collective-permute-start.6 = (bf16[512,256]{1,0:T(8,128)(2,1)S(1)}, bf16[512,256]{1,0:T(8,128)(2,1)S(1)}, u32[]{:S(2)}, u32[]{:S(2)}) collective-permute-start(bf16[512,256]{1,0:T(8,128)(2,1)S(1)} %collective-permute-done.5.refs_5_), channel_id=1, source_target_pairs={{0,32},{16,240},{32,64},{48,16},{64,96},{80,48},{96,128},{112,80},... | collective-permute-start | bytes 786440 | tf_op jit(solution)/shard_map/ppermute | solution.py:53
  17.0 13.3 %collective-permute-start.2 = (bf16[256,256]{1,0:T(8,128)(2,1)S(1)}, bf16[256,256]{1,0:T(8,128)(2,1)S(1)}, u32[]{:S(2)}, u32[]{:S(2)}) collective-permute-start(bf16[256,256]{1,0:T(8,128)(2,1)S(1)} %pad_maximum_fusion.2.refs_0_), channel_id=1, source_target_pairs={{0,128},{16,144},{32,160},{48,176},{64,192},{80,208},{96,224},{112... | collective-permute-start | bytes 393224 | tf_op jit(solution)/shard_map/ppermute | solution.py:52
  20.9 15.1 %collective-permute-start.8 = (bf16[512,256]{1,0:T(8,128)(2,1)S(1)}, bf16[512,256]{1,0:T(8,128)(2,1)S(1)}, u32[]{:S(2)}, u32[]{:S(2)}) collective-permute-start(bf16[512,256]{1,0:T(8,128)(2,1)S(1)} %collective-permute-done.5.refs_5_), channel_id=1, source_target_pairs={{0,16},{16,0},{32,48},{48,32},{64,80},{80,64},{96,112},{112,96},{1... | collective-permute-start | bytes 786440 | tf_op jit(solution)/shard_map/ppermute | solution.py:54
  20.9 15.1 %collective-permute-start.7 = (bf16[512,256]{1,0:T(8,128)(2,1)S(1)}, bf16[512,256]{1,0:T(8,128)(2,1)S(1)}, u32[]{:S(2)}, u32[]{:S(2)}) collective-permute-start(bf16[512,256]{1,0:T(8,128)(2,1)S(1)} %collective-permute-done.4.refs_4_), channel_id=1, source_target_pairs={{0,16},{16,0},{32,48},{48,32},{64,80},{80,64},{96,112},{112,96},{1... | collective-permute-start | bytes 786440 | tf_op jit(solution)/shard_map/ppermute | solution.py:54
  24.3 11.8 %collective-permute-start.9 = (bf16[512,256]{1,0:T(8,128)(2,1)S(1)}, bf16[512,256]{1,0:T(8,128)(2,1)S(1)}, u32[]{:S(2)}, u32[]{:S(2)}) collective-permute-start(bf16[512,256]{1,0:T(8,128)(2,1)S(1)} %collective-permute-done.6.refs_6_), channel_id=1, source_target_pairs={{0,16},{16,0},{32,48},{48,32},{64,80},{80,64},{96,112},{112,96},{1... | collective-permute-start | bytes 786440 | tf_op jit(solution)/shard_map/ppermute | solution.py:54
  25.3 10.7 %collective-permute-start = (bf16[128,512]{1,0:T(8,128)(2,1)S(1)}, bf16[128,512]{1,0:T(8,128)(2,1)S(1)}, u32[]{:S(2)}, u32[]{:S(2)}) collective-permute-start(bf16[128,512]{1,0:T(8,128)(2,1)S(1)} %get-tuple-element.34), channel_id=1, source_target_pairs={{0,16},{16,0},{32,48},{48,32},{64,80},{80,64},{96,112},{112,96},{1... | collective-permute-start | bytes 393224 | tf_op jit(solution)/shard_map/ppermute | solution.py:212
  30.3 5.7 %collective-permute-start.3 = (bf16[256,256]{1,0:T(8,128)(2,1)S(1)}, bf16[256,256]{1,0:T(8,128)(2,1)S(1)}, u32[]{:S(2)}, u32[]{:S(2)}) collective-permute-start(bf16[256,256]{1,0:T(8,128)(2,1)S(1)} %collective-permute-done.2.refs_2_), channel_id=1, source_target_pairs={{0,16},{16,0},{32,48},{48,32},{64,80},{80,64},{96,112},{112,96},{1... | collective-permute-start | bytes 393224 | tf_op jit(solution)/shard_map/ppermute | solution.py:55
  40.5 11.6 %collective-permute-start.16 = (bf16[4,128,512]{2,1,0:T(8,128)(2,1)S(1)}, bf16[4,128,512]{2,1,0:T(8,128)(2,1)S(1)}, u32[]{:S(2)}, u32[]{:S(2)}) collective-permute-start(bf16[4,128,512]{2,1,0:T(8,128)(2,1)S(1)} %get-tuple-element.22), channel_id=1, source_target_pairs={{0,8},{1,9},{2,10},{3,11},{4,12},{5,13},{6,14},{7,15},{8,0},{9,1},... | collective-permute-start | bytes 1572872 | tf_op jit(solution)/shard_map/ppermute | solution.py:196
  42.7 14.3 %collective-permute-start.17 = (bf16[4,128,512]{2,1,0:T(8,128)(2,1)S(1)}, bf16[4,128,512]{2,1,0:T(8,128)(2,1)S(1)}, u32[]{:S(2)}, u32[]{:S(2)}) collective-permute-start(bf16[4,128,512]{2,1,0:T(8,128)(2,1)S(1)} %get-tuple-element.23), channel_id=1, source_target_pairs={{0,4},{1,5},{2,6},{3,7},{4,8},{5,9},{6,10},{7,11},{8,12},{9,13},{1... | collective-permute-start | bytes 1572872 | tf_op jit(solution)/shard_map/ppermute | solution.py:196
  42.7 14.3 %collective-permute-start.18 = (bf16[4,128,512]{2,1,0:T(8,128)(2,1)S(1)}, bf16[4,128,512]{2,1,0:T(8,128)(2,1)S(1)}, u32[]{:S(2)}, u32[]{:S(2)}) collective-permute-start(bf16[4,128,512]{2,1,0:T(8,128)(2,1)S(1)} %get-tuple-element.24), channel_id=1, source_target_pairs={{0,12},{1,13},{2,14},{3,15},{4,0},{5,1},{6,2},{7,3},{8,4},{9,5},{1... | collective-permute-start | bytes 1572872 | tf_op jit(solution)/shard_map/ppermute | solution.py:196
  47.7 16.7 %collective-permute-start.10 = (bf16[4,128,512]{2,1,0:T(8,128)(2,1)S(1)}, bf16[4,128,512]{2,1,0:T(8,128)(2,1)S(1)}, u32[]{:S(2)}, u32[]{:S(2)}) collective-permute-start(bf16[4,128,512]{2,1,0:T(8,128)(2,1)S(1)} %get-tuple-element.18), channel_id=1, source_target_pairs={{0,8},{1,9},{2,10},{3,11},{4,12},{5,13},{6,14},{7,15},{8,0},{9,1},... | collective-permute-start | bytes 1572872 | tf_op jit(solution)/shard_map/ppermute | solution.py:196
  49.4 21.6 %collective-permute-start.11 = (bf16[4,128,512]{2,1,0:T(8,128)(2,1)S(1)}, bf16[4,128,512]{2,1,0:T(8,128)(2,1)S(1)}, u32[]{:S(2)}, u32[]{:S(2)}) collective-permute-start(bf16[4,128,512]{2,1,0:T(8,128)(2,1)S(1)} %get-tuple-element.19), channel_id=1, source_target_pairs={{0,4},{1,5},{2,6},{3,7},{4,8},{5,9},{6,10},{7,11},{8,12},{9,13},{1... | collective-permute-start | bytes 1572872 | tf_op jit(solution)/shard_map/ppermute | solution.py:196
  52.0 19.0 %collective-permute-start.12 = (bf16[4,128,512]{2,1,0:T(8,128)(2,1)S(1)}, bf16[4,128,512]{2,1,0:T(8,128)(2,1)S(1)}, u32[]{:S(2)}, u32[]{:S(2)}) collective-permute-start(bf16[4,128,512]{2,1,0:T(8,128)(2,1)S(1)} %get-tuple-element.20), channel_id=1, source_target_pairs={{0,12},{1,13},{2,14},{3,15},{4,0},{5,1},{6,2},{7,3},{8,4},{9,5},{1... | collective-permute-start | bytes 1572872 | tf_op jit(solution)/shard_map/ppermute | solution.py:196
  57.2 18.4 %collective-permute-start.19 = (bf16[128,512]{1,0:T(8,128)(2,1)S(1)}, bf16[128,512]{1,0:T(8,128)(2,1)S(1)}, u32[]{:S(2)}, u32[]{:S(2)}) collective-permute-start(bf16[128,512]{1,0:T(8,128)(2,1)S(1)} %get-tuple-element.30), channel_id=1, source_target_pairs={{0,2},{1,3},{2,0},{3,1},{4,6},{5,7},{6,4},{7,5},{8,10},{9,11},{10,... | collective-permute-start | bytes 393224 | tf_op jit(solution)/shard_map/ppermute | solution.py:198
  60.4 16.1 %collective-permute-start.21 = (bf16[128,512]{1,0:T(8,128)(2,1)S(1)}, bf16[128,512]{1,0:T(8,128)(2,1)S(1)}, u32[]{:S(2)}, u32[]{:S(2)}) collective-permute-start(bf16[128,512]{1,0:T(8,128)(2,1)S(1)} %get-tuple-element.31), channel_id=1, source_target_pairs={{0,3},{1,0},{2,1},{3,2},{4,7},{5,4},{6,5},{7,6},{8,11},{9,8},{10,9... | collective-permute-start | bytes 393224 | tf_op jit(solution)/shard_map/ppermute | solution.py:198
  64.4 12.2 %collective-permute-start.20 = (bf16[128,512]{1,0:T(8,128)(2,1)S(1)}, bf16[128,512]{1,0:T(8,128)(2,1)S(1)}, u32[]{:S(2)}, u32[]{:S(2)}) collective-permute-start(bf16[128,512]{1,0:T(8,128)(2,1)S(1)} %get-tuple-element.32), channel_id=1, source_target_pairs={{0,1},{1,2},{2,3},{3,0},{4,5},{5,6},{6,7},{7,4},{8,9},{9,10},{10,1... | collective-permute-start | bytes 393224 | tf_op jit(solution)/shard_map/ppermute | solution.py:198
  71.2 6.6 %collective-permute-start.13 = (bf16[128,512]{1,0:T(8,128)(2,1)S(1)}, bf16[128,512]{1,0:T(8,128)(2,1)S(1)}, u32[]{:S(2)}, u32[]{:S(2)}) collective-permute-start(bf16[128,512]{1,0:T(8,128)(2,1)S(1)} %get-tuple-element.27), channel_id=1, source_target_pairs={{0,2},{1,3},{2,0},{3,1},{4,6},{5,7},{6,4},{7,5},{8,10},{9,11},{10,... | collective-permute-start | bytes 393224 | tf_op jit(solution)/shard_map/ppermute | solution.py:198
  74.5 5.0 %collective-permute-start.15 = (bf16[128,512]{1,0:T(8,128)(2,1)S(1)}, bf16[128,512]{1,0:T(8,128)(2,1)S(1)}, u32[]{:S(2)}, u32[]{:S(2)}) collective-permute-start(bf16[128,512]{1,0:T(8,128)(2,1)S(1)} %get-tuple-element.28), channel_id=1, source_target_pairs={{0,3},{1,0},{2,1},{3,2},{4,7},{5,4},{6,5},{7,6},{8,11},{9,8},{10,9... | collective-permute-start | bytes 393224 | tf_op jit(solution)/shard_map/ppermute | solution.py:198
  75.6 6.2 %collective-permute-start.14 = (bf16[128,512]{1,0:T(8,128)(2,1)S(1)}, bf16[128,512]{1,0:T(8,128)(2,1)S(1)}, u32[]{:S(2)}, u32[]{:S(2)}) collective-permute-start(bf16[128,512]{1,0:T(8,128)(2,1)S(1)} %get-tuple-element.29), channel_id=1, source_target_pairs={{0,1},{1,2},{2,3},{3,0},{4,5},{5,6},{6,7},{7,4},{8,9},{9,10},{10,1... | collective-permute-start | bytes 393224 | tf_op jit(solution)/shard_map/ppermute | solution.py:198
  76.7 5.1 %collective-permute-start.22 = (bf16[128,512]{1,0:T(8,128)(2,1)S(1)}, bf16[128,512]{1,0:T(8,128)(2,1)S(1)}, u32[]{:S(2)}, u32[]{:S(2)}) collective-permute-start(bf16[128,512]{1,0:T(8,128)(2,1)S(1)} %fusion.2), channel_id=1, source_target_pairs={{0,16},{16,0},{32,48},{48,32},{64,80},{80,64},{96,112},{112,96},{1... | collective-permute-start | bytes 393224 | tf_op jit(solution)/shard_map/ppermute | solution.py:221

commit v2 on v1

--- a/solution.py
+++ b/solution.py
@@ -11,7 +11,7 @@
 HEAD_DIM = 128
 QUERY_GROUP = 8
 SPAN = 128
-CHUNK = 256
+CHUNK = 512
 NEG = -1e30
 NZ, NX, NY = 8, 4, 4
 FETCHES = 8
@@ -20,10 +20,10 @@
 SMEM = pl.BlockSpec(memory_space=pltpu.SMEM)
 HBM = pl.BlockSpec(memory_space=pltpu.HBM)
 BOTH = ("ctx", "grp")
-STEPS = (2, 1, 3)
+STEPS = (2, 1, 3, 0)
+HALF = SPAN // 2
 
 OTHER_CORE = [(i, i ^ 1) for i in range(2 * NZ)]
-FAR_SIDE = [(z * 2 + c, (z + 4) % NZ * 2 + c) for z in range(NZ) for c in range(2)]
 
 
 def ring(k):
@@ -40,19 +40,23 @@
     return pairs
 
 
+def sent(x, axis, pairs):
+    return lax.ppermute(x, axis, pairs)
+
+
 CAME = [(0, 0, 1), (0, 1, 1), (4, 0, 1), (4, 1, 1)]
 CAME += [(-k, 0, 2) for k in (1, 2, 3)] + [(k, 1, 2) for k in (1, 2, 3)]
 
 
 def gathered(own):
-    other = lax.ppermute(own, "ctx", OTHER_CORE)
+    other = sent(own, "ctx", OTHER_CORE)
     chip = jnp.concatenate([own, other], axis=0)
-    two = lax.ppermute(chip, "ctx", ring(2))
-    one = lax.ppermute(chip, "ctx", ring(1))
-    far = lax.ppermute(own, "ctx", FAR_SIDE)
-    three = lax.ppermute(two, "ctx", ring(1))
-    passed = [lax.ppermute(x, "ctx", OTHER_CORE) for x in (one, two, three)]
-    return [own, other, far, lax.ppermute(far, "ctx", OTHER_CORE), one, two, three] + passed
+    two = sent(chip, "ctx", ring(2))
+    one = sent(chip, "ctx", ring(1))
+    three = sent(two, "ctx", ring(1))
+    far = sent(two[: own.shape[0]], "ctx", ring(2))
+    passed = [sent(x, "ctx", OTHER_CORE) for x in (one, two, three)]
+    return [own, other, far, sent(far, "ctx", OTHER_CORE), one, two, three] + passed
 
 
 def block_of(where, k, j):
@@ -63,12 +67,28 @@
 
 
 def project(where, att, w_ref, outs):
+    up, down, up_add, down_add, kept = outs
     cols = w_ref.shape[1] // (NX * NY)
-    for k in STEPS + (0,):
+    top, low = slice(0, HALF), slice(HALF, SPAN)
+    for k in STEPS:
         for j in range(4):
             at = pl.multiple_of(block_of(where, k, j) * cols, cols)
             part = jnp.dot(att, w_ref[:, pl.ds(at, cols)], preferred_element_type=jnp.float32)
-            outs[k][j] = part.astype(jnp.bfloat16)
+            part = part.astype(jnp.bfloat16)
+            if k == 2:
+                up[0, j], down[0, j] = part[top], part[low]
+            elif k == 1:
+                up_add[j], up[1, j] = part[top], part[low]
+            elif k == 3:
+                down[1, j], down_add[j] = part[top], part[low]
+            else:
+                kept[j] = part
+
+
+def parcels(cols):
+    halves = jax.ShapeDtypeStruct((2, 4, HALF, cols), jnp.bfloat16)
+    half = jax.ShapeDtypeStruct((4, HALF, cols), jnp.bfloat16)
+    return [halves, halves, half, half, jax.ShapeDtypeStruct((4, SPAN, cols), jnp.bfloat16)]
 
 
 def fetch_kernel(where, w_hbm, w_ref, sems):
@@ -108,7 +128,7 @@
                 at = pl.multiple_of(where[6 + source * 2 + half] * SPAN, SPAN)
                 rows = slice((part * 2 + half) * SPAN, (part * 2 + half + 1) * SPAN)
                 keys[pl.ds(at, SPAN), :] = kv[rows, :HEAD_DIM]
-                values[pl.ds(at, SPAN), :] = kv[rows, HEAD_DIM:]
+                values[:, pl.ds(at, SPAN)] = kv[rows, HEAD_DIM:].T
 
 
 def attended(where, slot, q_ref, keys, values, acc):
@@ -116,7 +136,7 @@
     lanes = heads * SPAN
     scale = math.log2(math.e) / math.sqrt(HEAD_DIM)
     queries = jnp.concatenate(
-        [q_ref[:, h * HEAD_DIM : (h + 1) * HEAD_DIM] for h in range(heads)], axis=0
+        [q_ref[:, h * HEAD_DIM : (h + 1) * HEAD_DIM].T for h in range(heads)], axis=1
     )
     at = where[6 + slot] * SPAN
     pos = at + lax.broadcasted_iota(jnp.int32, (1, lanes), 1) % SPAN
@@ -127,28 +147,35 @@
     acc[...] = jnp.zeros_like(acc)
     kv_iota = lax.broadcasted_iota(jnp.int32, (CHUNK, lanes), 0)
 
-    def step(chunk, carry):
+    def step(chunk, carry, masked):
         top, total = carry
         rows = pl.ds(pl.multiple_of(chunk * CHUNK, CHUNK), CHUNK)
         scores = lax.dot_general(
-            keys[rows, :], queries, (((1,), (1,)), ((), ())), preferred_element_type=jnp.float32
+            keys[rows, :], queries, (((1,), (0,)), ((), ())), preferred_element_type=jnp.float32
         )
-        kv_pos = kv_iota + chunk * CHUNK
-        visible = (kv_pos >= low) & (kv_pos <= pos)
-        scores = jnp.where(visible, scores * scale, NEG)
+        scores = scores * scale
+        if masked:
+            kv_pos = kv_iota + chunk * CHUNK
+            visible = (kv_pos >= low) & (kv_pos <= pos)
+            scores = jnp.where(visible, scores, NEG)
         higher = jnp.maximum(top, jnp.max(scores, axis=0, keepdims=True))
         rescale = jnp.exp2(top - higher)
         probs = jnp.exp2(scores - higher)
         total = total * rescale + jnp.sum(probs, axis=0, keepdims=True)
-        mixed = lax.dot_general(
-            values[rows, :], probs.astype(jnp.bfloat16), (((0,), (0,)), ((), ())),
-            preferred_element_type=jnp.float32,
-        )
+        mixed = lax.dot_general(values[:, rows], probs.astype(jnp.bfloat16), (((1,), (0,)), ((), ())), preferred_element_type=jnp.float32)
         acc[...] = acc[...] * rescale + mixed
         return higher, total
 
-    start = (jnp.full((1, lanes), NEG, jnp.float32), jnp.zeros((1, lanes), jnp.float32))
-    _, total = lax.fori_loop(low0 // CHUNK, (at + SPAN - 1) // CHUNK + 1, step, start)
+    carry = (jnp.full((1, lanes), NEG, jnp.float32), jnp.zeros((1, lanes), jnp.float32))
+    low1 = jnp.int32(0)
+    for start in [where[i] for i in (3, 4, 5)]:
+        low1 = jnp.where(start <= at + SPAN - 1, start, low1)
+    begin, end = low0 // CHUNK, (at + SPAN - 1) // CHUNK + 1
+    whole = jnp.clip((low1 + CHUNK - 1) // CHUNK, begin, end - 1)
+    last = jnp.maximum(at // CHUNK, whole)
+    carry = lax.fori_loop(begin, whole, lambda c, s: step(c, s, True), carry)
+    carry = lax.fori_loop(whole, last, lambda c, s: step(c, s, False), carry)
+    _, total = lax.fori_loop(last, end, lambda c, s: step(c, s, True), carry)
     mixed = acc[...] / total
     return jnp.concatenate(
         [mixed[:, h * SPAN : (h + 1) * SPAN].T.astype(jnp.bfloat16) for h in range(heads)], axis=1
@@ -156,7 +183,7 @@
 
 
 def theirs_kernel(where, q_ref, w_ref, *refs):
-    kv_refs, (keys, values), outs, acc = refs[:-7], refs[-7:-5], refs[-5:-1], refs[-1]
+    kv_refs, (keys, values), outs, acc = refs[:-8], refs[-8:-6], refs[-6:-1], refs[-1]
     place(where, kv_refs, keys, values)
     ctx = where[0]
     slot = (ctx // 2 * 2 + 1 - ctx % 2) * 2 + ctx % 2
@@ -164,7 +191,7 @@
 
 
 def mine_kernel(where, q_ref, w_ref, keys, values, *refs):
-    outs, acc = refs[:4], refs[4]
+    outs, acc = refs[:5], refs[5]
     slot = where[0] * 2 + where[0] % 2
     project(where, attended(where, slot, q_ref, keys, values, acc), w_ref, outs)
 
@@ -172,13 +199,13 @@
 def attend(kernel, where, queries, weight, kv, seq, keep):
     width = queries.shape[1]
     cols = weight.shape[1] // (NX * NY)
-    kept = [jax.ShapeDtypeStruct((seq, HEAD_DIM), jnp.bfloat16)] * (2 * keep)
-    parts = [jax.ShapeDtypeStruct((4, SPAN, cols), jnp.bfloat16)] * 4
+    kept = [jax.ShapeDtypeStruct(d, jnp.bfloat16) for d in ((seq, HEAD_DIM), (HEAD_DIM, seq))] * keep
+    parts = parcels(cols)
     return pl.pallas_call(
         kernel,
         out_shape=kept + parts,
         in_specs=[SMEM] + [VMEM] * (2 + len(kv)),
-        out_specs=[VMEM] * (len(kept) + 4),
+        out_specs=[VMEM] * (len(kept) + len(parts)),
         scratch_shapes=[pltpu.VMEM((HEAD_DIM, width), jnp.float32)],
         compiler_params=pltpu.CompilerParams(vmem_limit_bytes=24 << 20),
         cost_estimate=pl.CostEstimate(
@@ -191,12 +218,57 @@
     return sum(p.astype(jnp.float32) for p in parts).astype(jnp.bfloat16)
 
 
+def combine_kernel(kept, up, down, up_sum, down_sum, *outs):
+    top, low = slice(0, HALF), slice(HALF, SPAN)
+    for j, out in enumerate(outs):
+        for rows, a, b in ((top, up_sum[j], down[1, j]), (low, up[1, j], down_sum[j])):
+            out[rows] = (
+                kept[j, rows].astype(jnp.float32) + a.astype(jnp.float32) + b.astype(jnp.float32)
+            ).astype(jnp.bfloat16)
+
+
+def combined(*parts):
+    rows, cols = parts[0].shape[1:]
+    return pl.pallas_call(
+        combine_kernel,
+        out_shape=[jax.ShapeDtypeStruct((rows, cols), jnp.bfloat16)] * 4,
+        in_specs=[VMEM] * 5,
+        out_specs=[VMEM] * 4,
+        compiler_params=pltpu.CompilerParams(vmem_limit_bytes=16 << 20),
+        cost_estimate=pl.CostEstimate(flops=1 << 20, bytes_accessed=2 << 20, transcendentals=0),
+        name="combine",
+    )(*parts)
+
+
 def reduced(parts):
-    got = [parts[0]]
-    got += [lax.ppermute(parts[k], BOTH, plane_steps(k, 0)) for k in STEPS]
-    line = [total_of([g[j] for g in got]) for j in range(4)]
-    last = [lax.ppermute(line[j], BOTH, plane_steps(j, 1)) for j in STEPS]
-    return total_of([line[0]] + last)
+    up, down, up_add, down_add, kept = parts
+    up = sent(up, BOTH, plane_steps(1, 0))
+    down = sent(down, BOTH, plane_steps(3, 0))
+    up_sum = sent(total_of([up_add, up[0]]), BOTH, plane_steps(1, 0))
+    down_sum = sent(total_of([down_add, down[0]]), BOTH, plane_steps(3, 0))
+    line = combined(kept, up, down, up_sum, down_sum)
+    last = [sent(line[j], BOTH, plane_steps(j, 1)) for j in (2, 1, 3)]
+    return [line[0]] + last
+
+
+def finish_kernel(where, back, a, b, c, d, out_ref):
+    core = where[0] % 2
+    total = a[...].astype(jnp.float32) + b[...].astype(jnp.float32)
+    total = total + c[...].astype(jnp.float32) + d[...].astype(jnp.float32)
+    out_ref[pl.ds(pl.multiple_of(core * SPAN, SPAN), SPAN), :] = total.astype(jnp.bfloat16)
+    out_ref[pl.ds(pl.multiple_of((1 - core) * SPAN, SPAN), SPAN), :] = back[...]
+
+
+def finished(where, back, terms):
+    return pl.pallas_call(
+        finish_kernel,
+        out_shape=jax.ShapeDtypeStruct((2 * SPAN, back.shape[1]), jnp.bfloat16),
+        in_specs=[SMEM] + [VMEM] * 5,
+        out_specs=VMEM,
+        compiler_params=pltpu.CompilerParams(vmem_limit_bytes=16 << 20),
+        cost_estimate=pl.CostEstimate(flops=1 << 18, bytes_accessed=1 << 20, transcendentals=0),
+        name="finish",
+    )(where, back, *terms)
 
 
 def shards(queries, keys, values, out_weight, span_order, document):
@@ -209,20 +281,19 @@
     )
     kept = lax.dynamic_slice_in_dim(queries, core * SPAN, SPAN, 0)
     away = lax.dynamic_slice_in_dim(queries, (1 - core) * SPAN, SPAN, 0)
-    swapped = lax.ppermute(away, "ctx", OTHER_CORE)
+    swapped = sent(away, "ctx", OTHER_CORE)
     starts = jnp.sum(document[None, :] < jnp.arange(1, 4)[:, None], axis=1, dtype=jnp.int32)
     index = jnp.stack([ctx, grp // NY, grp % NY]).astype(jnp.int32)
     where = jnp.concatenate([index, starts, span_order])
     weight = fetched(where, out_weight)
     blocks = gathered(own)
     seq = document.shape[0]
-    *kv, b0, b1, b2, b3 = attend(theirs_kernel, where, swapped, weight, blocks, seq, True)
+    *kv, up, down, up_add, down_add, own_part = attend(
+        theirs_kernel, where, swapped, weight, blocks, seq, True
+    )
     parts = attend(mine_kernel, where, kept, weight, kv, seq, False)
-    back = lax.ppermute(reduced([b0, b1, b2, b3]), "ctx", OTHER_CORE)
-    mine = reduced(parts)
-    return jnp.concatenate(
-        [jnp.where(core == 0, mine, back), jnp.where(core == 0, back, mine)], axis=0
-    )
+    back = sent(total_of(reduced([up, down, up_add, down_add, own_part])), "ctx", OTHER_CORE)
+    return finished(where, back, reduced(parts))
 
 
 def solution(mesh):

time: 82.9 us -> 76.9 us (0.928)
  the two profiles are of different devices: /device:TPU:2 before, /device:TPU:30 now
where the time goes in v2:
time: 76.9 us; the launch traced here: 76.7 us
  waiting for transfers between devices  30.5 us (40%)
  starting transfers between devices  29 us (38%)
  Pallas kernels  13 us (17%)
  local copies, waits for them, and re-layouts  2.61 us (3%)
  other arithmetic  1.32 us (2%)
    ppermute x25, waiting for transfers between devices, sent(): return lax.ppermute(x, axis, pairs)  30.5 us
    ppermute x25, starting transfers between devices, sent(): return lax.ppermute(x, axis, pairs)  29 us
    pallas_call x2, Pallas kernels, attend(): pl.pallas_call(kernel, out_shape=kept + parts, in_specs=[SMEM] + [VMEM] *...  7.32 us
    pallas_call x1, Pallas kernels, fetched(): pl.pallas_call(fetch_kernel, out_shape=jax.ShapeDtypeStruct(weight.shape,...  4.02 us
  transfers between devices with their start and end apart: 25, of which 12 were waited for; matrix products, arithmetic and copies ran while one was open for 4% of the time, Pallas kernels for 9%

profile of v2, /device:TPU:30, one launch (start us, length us, event | category | flops | bytes accessed | tf_op | source)
XLA Modules:
  0.0 76.7 jit_solution(10565376872402938961)
XLA Ops:
  0.0 0.9 %constant_dynamic-slice_fusion.1 = (bf16[256,128]{1,0:T(8,128)(2,1)S(1)}, bf16[256,128]{1,0:T(8,128)(2,1)S(1)}) fusion(bf16[256,1024]{1,0:T(8,128)(2,1)} %param.8, s32[]{:T(128)S(6)} %select_n.33, bf16[256,1024]{1,0:T(8,128)(2,1)} %param.7), kind=kLoop, calls=%fused_computation.17 | loop fusion | bytes 262148 | tf_op jit(solution)/shard_map/dynamic_slice | solution.py:280
  0.9 0.1 collective-permute-start.1
  1.0 1.3 %collective-permute-done.1.refs_1_ = bf16[256,256]{1,0:T(8,128)(2,1)S(1)} collective-permute-done((bf16[256,256]{1,0:T(8,128)(2,1)S(1)}, bf16[256,256]{1,0:T(8,128)(2,1)S(1)}, u32[]{:S(2)}, u32[]{:S(2)}) %collective-permute-start.1) | collective-permute-done | bytes 131104 | tf_op jit(solution)/shard_map/ppermute | solution.py:44
  2.4 3.3 %collective-permute-start.2 = (bf16[512,256]{1,0:T(8,128)(2,1)S(1)}, bf16[512,256]{1,0:T(8,128)(2,1)S(1)}, u32[]{:S(2)}, u32[]{:S(2)}) collective-permute-start(bf16[512,256]{1,0:T(8,128)(2,1)S(1)} %pad_maximum_fusion), channel_id=1, source_target_pairs={{0,64},{16,208},{32,96},{48,240},{64,128},{80,16},{96,160},{112,48... | collective-permute-start | bytes 786440 | tf_op jit(solution)/shard_map/ppermute | solution.py:44
  5.7 1.9 %collective-permute-start.5 = (bf16[512,256]{1,0:T(8,128)(2,1)S(1)}, bf16[512,256]{1,0:T(8,128)(2,1)S(1)}, u32[]{:S(2)}, u32[]{:S(2)}) collective-permute-start(bf16[512,256]{1,0:T(8,128)(2,1)S(1)} %pad_maximum_fusion), channel_id=1, source_target_pairs={{0,32},{16,240},{32,64},{48,16},{64,96},{80,48},{96,128},{112,80},... | collective-permute-start | bytes 786440 | tf_op jit(solution)/shard_map/ppermute | solution.py:44
  7.6 6.1 %collective-permute-done.2.refs_5_ = bf16[512,256]{1,0:T(8,128)(2,1)S(1)} collective-permute-done((bf16[512,256]{1,0:T(8,128)(2,1)S(1)}, bf16[512,256]{1,0:T(8,128)(2,1)S(1)}, u32[]{:S(2)}, u32[]{:S(2)}) %collective-permute-start.2) | collective-permute-done | bytes 262176 | tf_op jit(solution)/shard_map/ppermute | solution.py:44
  13.7 3.3 %collective-permute-start.6 = (bf16[512,256]{1,0:T(8,128)(2,1)S(1)}, bf16[512,256]{1,0:T(8,128)(2,1)S(1)}, u32[]{:S(2)}, u32[]{:S(2)}) collective-permute-start(bf16[512,256]{1,0:T(8,128)(2,1)S(1)} %collective-permute-done.2.refs_5_), channel_id=1, source_target_pairs={{0,32},{16,240},{32,64},{48,16},{64,96},{80,48},{96,128},{112,80},... | collective-permute-start | bytes 786440 | tf_op jit(solution)/shard_map/ppermute | solution.py:44
  17.0 0.4 collective-permute-start.3
  17.5 1.5 %collective-permute-start.8 = (bf16[512,256]{1,0:T(8,128)(2,1)S(1)}, bf16[512,256]{1,0:T(8,128)(2,1)S(1)}, u32[]{:S(2)}, u32[]{:S(2)}) collective-permute-start(bf16[512,256]{1,0:T(8,128)(2,1)S(1)} %collective-permute-done.2.refs_5_), channel_id=1, source_target_pairs={{0,16},{16,0},{32,48},{48,32},{64,80},{80,64},{96,112},{112,96},{1... | collective-permute-start | bytes 786440 | tf_op jit(solution)/shard_map/ppermute | solution.py:44
  19.0 0.0 collective-permute-done.5.refs_4_
  19.0 0.0 collective-permute-start.7
  19.0 3.5 %collective-permute-done.6.refs_6_ = bf16[512,256]{1,0:T(8,128)(2,1)S(1)} collective-permute-done((bf16[512,256]{1,0:T(8,128)(2,1)S(1)}, bf16[512,256]{1,0:T(8,128)(2,1)S(1)}, u32[]{:S(2)}, u32[]{:S(2)}) %collective-permute-start.6) | collective-permute-done | bytes 262176 | tf_op jit(solution)/shard_map/ppermute | solution.py:44
  22.4 0.0 collective-permute-start.9
  22.4 1.0 %constant_dynamic-slice_fusion = (bf16[128,512]{1,0:T(8,128)(2,1)S(1)}, bf16[128,512]{1,0:T(8,128)(2,1)S(1)}) fusion(bf16[256,512]{1,0:T(8,128)(2,1)} %param.6, s32[]{:T(128)S(6)} %select_n.34, s32[]{:T(128)S(6)} %select_n.31), kind=kLoop, calls=%fused_computation.16 | loop fusion | bytes 524296 | tf_op jit(solution)/shard_map/dynamic_slice | solution.py:282
  23.4 0.6 collective-permute-start
  24.0 1.9 %collective-permute-done.3.refs_2_ = bf16[256,256]{1,0:T(8,128)(2,1)S(1)} collective-permute-done((bf16[256,256]{1,0:T(8,128)(2,1)S(1)}, bf16[256,256]{1,0:T(8,128)(2,1)S(1)}, u32[]{:S(2)}, u32[]{:S(2)}) %collective-permute-start.3) | collective-permute-done | bytes 131104 | tf_op jit(solution)/shard_map/ppermute | solution.py:44
  25.9 0.0 collective-permute-start.4
  25.9 0.9 %convert_reduce_fusion = s32[3]{0:T(128)S(1)} fusion(s32[4096]{0:T(1024)} %param.11, s32[3]{0:T(128)S(1)} %iota_add_fusion), kind=kLoop, calls=%fused_computation.15 | loop fusion | flops 36861 | bytes 16408 | tf_op jit(solution)/shard_map/reduce_sum | solution.py:285
  26.8 0.7 concatenate.9.where
  27.6 4.0 %fetch.1.w_ref = bf16[512,8192]{1,0:T(8,128)(2,1)S(1)} custom-call(s32[38]{0:T(128)S(1)} %concatenate.9.where, bf16[512,8192]{1,0:T(8,128)(2,1)} %w_hbm.1), custom_call_target="tpu_custom_call" | custom-call | bytes 16777216 | tf_op jit(solution)/shard_map/fetch/pallas_call | solution.py:109
  31.6 0.0 collective-permute-done.q_ref
  31.6 0.0 collective-permute-done.7.refs_7_
  31.6 0.0 collective-permute-done.4.refs_3_
  31.6 0.0 collective-permute-done.8.refs_8_
  31.6 0.0 collective-permute-done.9.refs_9_
  31.6 4.5 %shard_map.64 = (bf16[4096,128]{1,0:T(8,128)(2,1)S(1)}, bf16[128,4096]{1,0:T(8,128)(2,1)S(1)}, bf16[2,4,64,512]{3,2,1,0:T(8,128)(2,1)S(1)}, bf16[2,4,64,512]{3,2...) custom-call(s32[38]{0:T(128)S(1)} %concatenate.9.where, ...), custom_call_target="tpu_custom_call" | custom-call | flops 2147483648 | bytes 12582912 | tf_op jit(solution)/shard_map/pallas_call | solution.py:204
  36.2 0.5 collective-permute-start.10
  36.7 1.6 %collective-permute-start.11 = (bf16[2,4,64,512]{3,2,1,0:T(8,128)(2,1)S(1)}, bf16[2,4,64,512]{3,2,1,0:T(8,128)(2,1)S(1)}, u32[]{:S(2)}, u32[]{:S(2)}) collective-permute-start(bf16[2,4,64,512]{3,2,1,0:T(8,128)(2,1)S(1)} %get-tuple-element.27), channel_id=1, source_target_pairs={{0,12},{1,13},{2,14},{3,15},{4,0},{5,1},{6,2},{7,3},{8,4},{9,5},{1... | collective-permute-start | bytes 1572872 | tf_op jit(solution)/shard_map/ppermute | solution.py:44
  38.3 2.8 %shard_map.65 = (bf16[2,4,64,512]{3,2,1,0:T(8,128)(2,1)S(1)}, bf16[2,4,64,512]{3,2,1,0:T(8,128)(2,1)S(1)}, bf16[4,64,512]{2,1,0:T(8,128)(2,1)S(1)}, bf16[4,64,51...) custom-call(s32[38]{0:T(128)S(1)} %concatenate.9.where, bf16[128,512]{1,0:T(8,128)(2,1)S(1)} %get-tuple-element.45.q_ref, ...), custom_call_target="tpu_custom_call" | custom-call | flops 2147483648 | bytes 12582912 | tf_op jit(solution)/shard_map/pallas_call | solution.py:204
  41.1 1.7 %collective-permute-start.18 = (bf16[2,4,64,512]{3,2,1,0:T(8,128)(2,1)S(1)}, bf16[2,4,64,512]{3,2,1,0:T(8,128)(2,1)S(1)}, u32[]{:S(2)}, u32[]{:S(2)}) collective-permute-start(bf16[2,4,64,512]{3,2,1,0:T(8,128)(2,1)S(1)} %get-tuple-element.37), channel_id=1, source_target_pairs={{0,4},{1,5},{2,6},{3,7},{4,8},{5,9},{6,10},{7,11},{8,12},{9,13},{1... | collective-permute-start | bytes 1572872 | tf_op jit(solution)/shard_map/ppermute | solution.py:44
  42.8 0.4 collective-permute-start.19
  43.2 2.2 %collective-permute-done.10.up = bf16[2,4,64,512]{3,2,1,0:T(8,128)(2,1)S(1)} collective-permute-done((bf16[2,4,64,512]{3,2,1,0:T(8,128)(2,1)S(1)}, bf16[2,4,64,512]{3,2,1,0:T(8,128)(2,1)S(1)}, u32[]{:S(2)}, u32[]{:S(2)}) %collective-permute-start.10) | collective-permute-done | bytes 524320 | tf_op jit(solution)/shard_map/ppermute | solution.py:44
  45.4 0.1 fusion.3
  45.5 1.7 %collective-permute-start.12 = (bf16[4,64,512]{2,1,0:T(8,128)(2,1)S(1)}, bf16[4,64,512]{2,1,0:T(8,128)(2,1)S(1)}, u32[]{:S(2)}, u32[]{:S(2)}) collective-permute-start(bf16[4,64,512]{2,1,0:T(8,128)(2,1)S(1)} %fusion.3), channel_id=1, source_target_pairs={{0,4},{1,5},{2,6},{3,7},{4,8},{5,9},{6,10},{7,11},{8,12},{9,13},{1... | collective-permute-start | bytes 786440 | tf_op jit(solution)/shard_map/ppermute | solution.py:44
  47.2 0.0 collective-permute-done.11.down
  47.2 0.1 fusion.2
  47.3 0.4 collective-permute-start.13
  47.7 3.3 %collective-permute-done.18.up = bf16[2,4,64,512]{3,2,1,0:T(8,128)(2,1)S(1)} collective-permute-done((bf16[2,4,64,512]{3,2,1,0:T(8,128)(2,1)S(1)}, bf16[2,4,64,512]{3,2,1,0:T(8,128)(2,1)S(1)}, u32[]{:S(2)}, u32[]{:S(2)}) %collective-permute-start.18) | collective-permute-done | bytes 524320 | tf_op jit(solution)/shard_map/ppermute | solution.py:44
  51.0 0.1 fusion.1
  51.1 2.3 %collective-permute-start.20 = (bf16[4,64,512]{2,1,0:T(8,128)(2,1)S(1)}, bf16[4,64,512]{2,1,0:T(8,128)(2,1)S(1)}, u32[]{:S(2)}, u32[]{:S(2)}) collective-permute-start(bf16[4,64,512]{2,1,0:T(8,128)(2,1)S(1)} %fusion.1), channel_id=1, source_target_pairs={{0,4},{1,5},{2,6},{3,7},{4,8},{5,9},{6,10},{7,11},{8,12},{9,13},{1... | collective-permute-start | bytes 786440 | tf_op jit(solution)/shard_map/ppermute | solution.py:44
  53.4 0.0 collective-permute-done.19.down
  53.4 0.1 fusion
  53.4 0.1 collective-permute-start.21
  53.5 0.3 collective-permute-done.12.up_sum
  53.8 2.2 %collective-permute-done.13.down_sum = bf16[4,64,512]{2,1,0:T(8,128)(2,1)S(1)} collective-permute-done((bf16[4,64,512]{2,1,0:T(8,128)(2,1)S(1)}, bf16[4,64,512]{2,1,0:T(8,128)(2,1)S(1)}, u32[]{:S(2)}, u32[]{:S(2)}) %collective-permute-start.13) | collective-permute-done | bytes 262176 | tf_op jit(solution)/shard_map/ppermute | solution.py:44
  56.0 0.2 combine.2
  56.2 1.3 %collective-permute-start.14 = (bf16[128,512]{1,0:T(8,128)(2,1)S(1)}, bf16[128,512]{1,0:T(8,128)(2,1)S(1)}, u32[]{:S(2)}, u32[]{:S(2)}) collective-permute-start(bf16[128,512]{1,0:T(8,128)(2,1)S(1)} %get-tuple-element.31), channel_id=1, source_target_pairs={{0,2},{1,3},{2,0},{3,1},{4,6},{5,7},{6,4},{7,5},{8,10},{9,11},{10,... | collective-permute-start | bytes 393224 | tf_op jit(solution)/shard_map/ppermute | solution.py:44
  57.5 2.2 %collective-permute-start.15 = (bf16[128,512]{1,0:T(8,128)(2,1)S(1)}, bf16[128,512]{1,0:T(8,128)(2,1)S(1)}, u32[]{:S(2)}, u32[]{:S(2)}) collective-permute-start(bf16[128,512]{1,0:T(8,128)(2,1)S(1)} %get-tuple-element.32), channel_id=1, source_target_pairs={{0,1},{1,2},{2,3},{3,0},{4,5},{5,6},{6,7},{7,4},{8,9},{9,10},{10,1... | collective-permute-start | bytes 393224 | tf_op jit(solution)/shard_map/ppermute | solution.py:44
  59.7 0.0 collective-permute-start.16
  59.7 0.0 collective-permute-done.20.up_sum
  59.7 3.8 %collective-permute-done.21.down_sum = bf16[4,64,512]{2,1,0:T(8,128)(2,1)S(1)} collective-permute-done((bf16[4,64,512]{2,1,0:T(8,128)(2,1)S(1)}, bf16[4,64,512]{2,1,0:T(8,128)(2,1)S(1)}, u32[]{:S(2)}, u32[]{:S(2)}) %collective-permute-start.21) | collective-permute-done | bytes 262176 | tf_op jit(solution)/shard_map/ppermute | solution.py:44
  63.5 0.2 combine.3
  63.7 3.1 %collective-permute-start.22 = (bf16[128,512]{1,0:T(8,128)(2,1)S(1)}, bf16[128,512]{1,0:T(8,128)(2,1)S(1)}, u32[]{:S(2)}, u32[]{:S(2)}) collective-permute-start(bf16[128,512]{1,0:T(8,128)(2,1)S(1)} %get-tuple-element.42), channel_id=1, source_target_pairs={{0,2},{1,3},{2,0},{3,1},{4,6},{5,7},{6,4},{7,5},{8,10},{9,11},{10,... | collective-permute-start | bytes 393224 | tf_op jit(solution)/shard_map/ppermute | solution.py:44
  66.8 2.4 %collective-permute-start.23 = (bf16[128,512]{1,0:T(8,128)(2,1)S(1)}, bf16[128,512]{1,0:T(8,128)(2,1)S(1)}, u32[]{:S(2)}, u32[]{:S(2)}) collective-permute-start(bf16[128,512]{1,0:T(8,128)(2,1)S(1)} %get-tuple-element.43), channel_id=1, source_target_pairs={{0,1},{1,2},{2,3},{3,0},{4,5},{5,6},{6,7},{7,4},{8,9},{9,10},{10,1... | collective-permute-start | bytes 393224 | tf_op jit(solution)/shard_map/ppermute | solution.py:44
  69.2 0.0 collective-permute-done.14
  69.2 0.0 collective-permute-start.24
  69.2 0.0 collective-permute-done.16
  69.2 0.1 add_convert_fusion
  69.3 0.1 collective-permute-start.17
  69.4 0.9 %collective-permute-done.22.b = bf16[128,512]{1,0:T(8,128)(2,1)S(1)} collective-permute-done((bf16[128,512]{1,0:T(8,128)(2,1)S(1)}, bf16[128,512]{1,0:T(8,128)(2,1)S(1)}, u32[]{:S(2)}, u32[]{:S(2)}) %collective-permute-start.22) | collective-permute-done | bytes 131104 | tf_op jit(solution)/shard_map/ppermute | solution.py:44
  70.2 1.5 %collective-permute-done.23.c = bf16[128,512]{1,0:T(8,128)(2,1)S(1)} collective-permute-done((bf16[128,512]{1,0:T(8,128)(2,1)S(1)}, bf16[128,512]{1,0:T(8,128)(2,1)S(1)}, u32[]{:S(2)}, u32[]{:S(2)}) %collective-permute-start.23) | collective-permute-done | bytes 131104 | tf_op jit(solution)/shard_map/ppermute | solution.py:44
  71.7 3.6 %collective-permute-done.24.d = bf16[128,512]{1,0:T(8,128)(2,1)S(1)} collective-permute-done((bf16[128,512]{1,0:T(8,128)(2,1)S(1)}, bf16[128,512]{1,0:T(8,128)(2,1)S(1)}, u32[]{:S(2)}, u32[]{:S(2)}) %collective-permute-start.24) | collective-permute-done | bytes 131104 | tf_op jit(solution)/shard_map/ppermute | solution.py:44
  75.3 0.0 collective-permute-done.17.back
  75.3 1.3 %finish.1 = bf16[256,512]{1,0:T(8,128)(2,1)} custom-call(s32[38]{0:T(128)S(1)} %concatenate.9.where, bf16[128,512]{1,0:T(8,128)(2,1)S(1)} %collective-permute-done.17.back, bf16[128,512]{1,0:T(8,128)(2,1)S(1)} %get-tuple-element.41.a, bf16[128,512]{1,0:T(8,128)(2,1)S(1)} %collective-permute-done.22.b, bf16[128,512]{1,0:T(8,128)(2,1)S(1)} %collective-permute-done.23.c, ...), custom_call_target="tpu_custom_call" | custom-call | flops 262144 | bytes 1048576 | tf_op jit(solution)/shard_map/finish/pallas_call | solution.py:263
  (5 shorter events, 0.1 us)
Async XLA Ops:
  0.9 1.4 %collective-permute-start.1 = (bf16[256,256]{1,0:T(8,128)(2,1)S(1)}, bf16[256,256]{1,0:T(8,128)(2,1)S(1)}, u32[]{:S(2)}, u32[]{:S(2)}) collective-permute-start(bf16[256,256]{1,0:T(8,128)(2,1)S(1)} %pad_maximum_fusion.1.refs_0_), channel_id=1, source_target_pairs={{0,16},{16,0},{32,48},{48,32},{64,80},{80,64},{96,112},{112,96},{1... | collective-permute-start | bytes 393224 | tf_op jit(solution)/shard_map/ppermute | solution.py:44
  2.4 11.3 %collective-permute-start.2 = (bf16[512,256]{1,0:T(8,128)(2,1)S(1)}, bf16[512,256]{1,0:T(8,128)(2,1)S(1)}, u32[]{:S(2)}, u32[]{:S(2)}) collective-permute-start(bf16[512,256]{1,0:T(8,128)(2,1)S(1)} %pad_maximum_fusion), channel_id=1, source_target_pairs={{0,64},{16,208},{32,96},{48,240},{64,128},{80,16},{96,160},{112,48... | collective-permute-start | bytes 786440 | tf_op jit(solution)/shard_map/ppermute | solution.py:44
  5.7 13.2 %collective-permute-start.5 = (bf16[512,256]{1,0:T(8,128)(2,1)S(1)}, bf16[512,256]{1,0:T(8,128)(2,1)S(1)}, u32[]{:S(2)}, u32[]{:S(2)}) collective-permute-start(bf16[512,256]{1,0:T(8,128)(2,1)S(1)} %pad_maximum_fusion), channel_id=1, source_target_pairs={{0,32},{16,240},{32,64},{48,16},{64,96},{80,48},{96,128},{112,80},... | collective-permute-start | bytes 786440 | tf_op jit(solution)/shard_map/ppermute | solution.py:44
  13.7 8.7 %collective-permute-start.6 = (bf16[512,256]{1,0:T(8,128)(2,1)S(1)}, bf16[512,256]{1,0:T(8,128)(2,1)S(1)}, u32[]{:S(2)}, u32[]{:S(2)}) collective-permute-start(bf16[512,256]{1,0:T(8,128)(2,1)S(1)} %collective-permute-done.2.refs_5_), channel_id=1, source_target_pairs={{0,32},{16,240},{32,64},{48,16},{64,96},{80,48},{96,128},{112,80},... | collective-permute-start | bytes 786440 | tf_op jit(solution)/shard_map/ppermute | solution.py:44
  17.0 8.8 %collective-permute-start.3 = (bf16[256,256]{1,0:T(8,128)(2,1)S(1)}, bf16[256,256]{1,0:T(8,128)(2,1)S(1)}, u32[]{:S(2)}, u32[]{:S(2)}) collective-permute-start(bf16[256,256]{1,0:T(8,128)(2,1)S(1)} %slice.20), channel_id=1, source_target_pairs={{0,64},{16,208},{32,96},{48,240},{64,128},{80,16},{96,160},{112,48... | collective-permute-start | bytes 393224 | tf_op jit(solution)/shard_map/ppermute | solution.py:44
  17.5 14.2 %collective-permute-start.8 = (bf16[512,256]{1,0:T(8,128)(2,1)S(1)}, bf16[512,256]{1,0:T(8,128)(2,1)S(1)}, u32[]{:S(2)}, u32[]{:S(2)}) collective-permute-start(bf16[512,256]{1,0:T(8,128)(2,1)S(1)} %collective-permute-done.2.refs_5_), channel_id=1, source_target_pairs={{0,16},{16,0},{32,48},{48,32},{64,80},{80,64},{96,112},{112,96},{1... | collective-permute-start | bytes 786440 | tf_op jit(solution)/shard_map/ppermute | solution.py:44
  19.0 12.6 %collective-permute-start.7 = (bf16[512,256]{1,0:T(8,128)(2,1)S(1)}, bf16[512,256]{1,0:T(8,128)(2,1)S(1)}, u32[]{:S(2)}, u32[]{:S(2)}) collective-permute-start(bf16[512,256]{1,0:T(8,128)(2,1)S(1)} %collective-permute-done.5.refs_4_), channel_id=1, source_target_pairs={{0,16},{16,0},{32,48},{48,32},{64,80},{80,64},{96,112},{112,96},{1... | collective-permute-start | bytes 786440 | tf_op jit(solution)/shard_map/ppermute | solution.py:44
  22.4 9.2 %collective-permute-start.9 = (bf16[512,256]{1,0:T(8,128)(2,1)S(1)}, bf16[512,256]{1,0:T(8,128)(2,1)S(1)}, u32[]{:S(2)}, u32[]{:S(2)}) collective-permute-start(bf16[512,256]{1,0:T(8,128)(2,1)S(1)} %collective-permute-done.6.refs_6_), channel_id=1, source_target_pairs={{0,16},{16,0},{32,48},{48,32},{64,80},{80,64},{96,112},{112,96},{1... | collective-permute-start | bytes 786440 | tf_op jit(solution)/shard_map/ppermute | solution.py:44
  23.4 8.2 %collective-permute-start = (bf16[128,512]{1,0:T(8,128)(2,1)S(1)}, bf16[128,512]{1,0:T(8,128)(2,1)S(1)}, u32[]{:S(2)}, u32[]{:S(2)}) collective-permute-start(bf16[128,512]{1,0:T(8,128)(2,1)S(1)} %get-tuple-element.46), channel_id=1, source_target_pairs={{0,16},{16,0},{32,48},{48,32},{64,80},{80,64},{96,112},{112,96},{1... | collective-permute-start | bytes 393224 | tf_op jit(solution)/shard_map/ppermute | solution.py:44
  25.9 5.7 %collective-permute-start.4 = (bf16[256,256]{1,0:T(8,128)(2,1)S(1)}, bf16[256,256]{1,0:T(8,128)(2,1)S(1)}, u32[]{:S(2)}, u32[]{:S(2)}) collective-permute-start(bf16[256,256]{1,0:T(8,128)(2,1)S(1)} %collective-permute-done.3.refs_2_), channel_id=1, source_target_pairs={{0,16},{16,0},{32,48},{48,32},{64,80},{80,64},{96,112},{112,96},{1... | collective-permute-start | bytes 393224 | tf_op jit(solution)/shard_map/ppermute | solution.py:44
  36.2 9.3 %collective-permute-start.10 = (bf16[2,4,64,512]{3,2,1,0:T(8,128)(2,1)S(1)}, bf16[2,4,64,512]{3,2,1,0:T(8,128)(2,1)S(1)}, u32[]{:S(2)}, u32[]{:S(2)}) collective-permute-start(bf16[2,4,64,512]{3,2,1,0:T(8,128)(2,1)S(1)} %get-tuple-element.26), channel_id=1, source_target_pairs={{0,4},{1,5},{2,6},{3,7},{4,8},{5,9},{6,10},{7,11},{8,12},{9,13},{1... | collective-permute-start | bytes 1572872 | tf_op jit(solution)/shard_map/ppermute | solution.py:44
  36.7 10.5 %collective-permute-start.11 = (bf16[2,4,64,512]{3,2,1,0:T(8,128)(2,1)S(1)}, bf16[2,4,64,512]{3,2,1,0:T(8,128)(2,1)S(1)}, u32[]{:S(2)}, u32[]{:S(2)}) collective-permute-start(bf16[2,4,64,512]{3,2,1,0:T(8,128)(2,1)S(1)} %get-tuple-element.27), channel_id=1, source_target_pairs={{0,12},{1,13},{2,14},{3,15},{4,0},{5,1},{6,2},{7,3},{8,4},{9,5},{1... | collective-permute-start | bytes 1572872 | tf_op jit(solution)/shard_map/ppermute | solution.py:44
  41.1 10.0 %collective-permute-start.18 = (bf16[2,4,64,512]{3,2,1,0:T(8,128)(2,1)S(1)}, bf16[2,4,64,512]{3,2,1,0:T(8,128)(2,1)S(1)}, u32[]{:S(2)}, u32[]{:S(2)}) collective-permute-start(bf16[2,4,64,512]{3,2,1,0:T(8,128)(2,1)S(1)} %get-tuple-element.37), channel_id=1, source_target_pairs={{0,4},{1,5},{2,6},{3,7},{4,8},{5,9},{6,10},{7,11},{8,12},{9,13},{1... | collective-permute-start | bytes 1572872 | tf_op jit(solution)/shard_map/ppermute | solution.py:44
  42.8 10.5 %collective-permute-start.19 = (bf16[2,4,64,512]{3,2,1,0:T(8,128)(2,1)S(1)}, bf16[2,4,64,512]{3,2,1,0:T(8,128)(2,1)S(1)}, u32[]{:S(2)}, u32[]{:S(2)}) collective-permute-start(bf16[2,4,64,512]{3,2,1,0:T(8,128)(2,1)S(1)} %get-tuple-element.38), channel_id=1, source_target_pairs={{0,12},{1,13},{2,14},{3,15},{4,0},{5,1},{6,2},{7,3},{8,4},{9,5},{1... | collective-permute-start | bytes 1572872 | tf_op jit(solution)/shard_map/ppermute | solution.py:44
  45.5 8.4 %collective-permute-start.12 = (bf16[4,64,512]{2,1,0:T(8,128)(2,1)S(1)}, bf16[4,64,512]{2,1,0:T(8,128)(2,1)S(1)}, u32[]{:S(2)}, u32[]{:S(2)}) collective-permute-start(bf16[4,64,512]{2,1,0:T(8,128)(2,1)S(1)} %fusion.3), channel_id=1, source_target_pairs={{0,4},{1,5},{2,6},{3,7},{4,8},{5,9},{6,10},{7,11},{8,12},{9,13},{1... | collective-permute-start | bytes 786440 | tf_op jit(solution)/shard_map/ppermute | solution.py:44
  47.3 8.7 %collective-permute-start.13 = (bf16[4,64,512]{2,1,0:T(8,128)(2,1)S(1)}, bf16[4,64,512]{2,1,0:T(8,128)(2,1)S(1)}, u32[]{:S(2)}, u32[]{:S(2)}) collective-permute-start(bf16[4,64,512]{2,1,0:T(8,128)(2,1)S(1)} %fusion.2), channel_id=1, source_target_pairs={{0,12},{1,13},{2,14},{3,15},{4,0},{5,1},{6,2},{7,3},{8,4},{9,5},{1... | collective-permute-start | bytes 786440 | tf_op jit(solution)/shard_map/ppermute | solution.py:44
  51.1 8.6 %collective-permute-start.20 = (bf16[4,64,512]{2,1,0:T(8,128)(2,1)S(1)}, bf16[4,64,512]{2,1,0:T(8,128)(2,1)S(1)}, u32[]{:S(2)}, u32[]{:S(2)}) collective-permute-start(bf16[4,64,512]{2,1,0:T(8,128)(2,1)S(1)} %fusion.1), channel_id=1, source_target_pairs={{0,4},{1,5},{2,6},{3,7},{4,8},{5,9},{6,10},{7,11},{8,12},{9,13},{1... | collective-permute-start | bytes 786440 | tf_op jit(solution)/shard_map/ppermute | solution.py:44
  53.4 10.0 %collective-permute-start.21 = (bf16[4,64,512]{2,1,0:T(8,128)(2,1)S(1)}, bf16[4,64,512]{2,1,0:T(8,128)(2,1)S(1)}, u32[]{:S(2)}, u32[]{:S(2)}) collective-permute-start(bf16[4,64,512]{2,1,0:T(8,128)(2,1)S(1)} %fusion), channel_id=1, source_target_pairs={{0,12},{1,13},{2,14},{3,15},{4,0},{5,1},{6,2},{7,3},{8,4},{9,5},{1... | collective-permute-start | bytes 786440 | tf_op jit(solution)/shard_map/ppermute | solution.py:44
  56.2 12.9 %collective-permute-start.14 = (bf16[128,512]{1,0:T(8,128)(2,1)S(1)}, bf16[128,512]{1,0:T(8,128)(2,1)S(1)}, u32[]{:S(2)}, u32[]{:S(2)}) collective-permute-start(bf16[128,512]{1,0:T(8,128)(2,1)S(1)} %get-tuple-element.31), channel_id=1, source_target_pairs={{0,2},{1,3},{2,0},{3,1},{4,6},{5,7},{6,4},{7,5},{8,10},{9,11},{10,... | collective-permute-start | bytes 393224 | tf_op jit(solution)/shard_map/ppermute | solution.py:44
  57.5 11.6 %collective-permute-start.15 = (bf16[128,512]{1,0:T(8,128)(2,1)S(1)}, bf16[128,512]{1,0:T(8,128)(2,1)S(1)}, u32[]{:S(2)}, u32[]{:S(2)}) collective-permute-start(bf16[128,512]{1,0:T(8,128)(2,1)S(1)} %get-tuple-element.32), channel_id=1, source_target_pairs={{0,1},{1,2},{2,3},{3,0},{4,5},{5,6},{6,7},{7,4},{8,9},{9,10},{10,1... | collective-permute-start | bytes 393224 | tf_op jit(solution)/shard_map/ppermute | solution.py:44
  59.7 9.5 %collective-permute-start.16 = (bf16[128,512]{1,0:T(8,128)(2,1)S(1)}, bf16[128,512]{1,0:T(8,128)(2,1)S(1)}, u32[]{:S(2)}, u32[]{:S(2)}) collective-permute-start(bf16[128,512]{1,0:T(8,128)(2,1)S(1)} %get-tuple-element.33), channel_id=1, source_target_pairs={{0,3},{1,0},{2,1},{3,2},{4,7},{5,4},{6,5},{7,6},{8,11},{9,8},{10,9... | collective-permute-start | bytes 393224 | tf_op jit(solution)/shard_map/ppermute | solution.py:44
  63.7 6.6 %collective-permute-start.22 = (bf16[128,512]{1,0:T(8,128)(2,1)S(1)}, bf16[128,512]{1,0:T(8,128)(2,1)S(1)}, u32[]{:S(2)}, u32[]{:S(2)}) collective-permute-start(bf16[128,512]{1,0:T(8,128)(2,1)S(1)} %get-tuple-element.42), channel_id=1, source_target_pairs={{0,2},{1,3},{2,0},{3,1},{4,6},{5,7},{6,4},{7,5},{8,10},{9,11},{10,... | collective-permute-start | bytes 393224 | tf_op jit(solution)/shard_map/ppermute | solution.py:44
  66.8 5.0 %collective-permute-start.23 = (bf16[128,512]{1,0:T(8,128)(2,1)S(1)}, bf16[128,512]{1,0:T(8,128)(2,1)S(1)}, u32[]{:S(2)}, u32[]{:S(2)}) collective-permute-start(bf16[128,512]{1,0:T(8,128)(2,1)S(1)} %get-tuple-element.43), channel_id=1, source_target_pairs={{0,1},{1,2},{2,3},{3,0},{4,5},{5,6},{6,7},{7,4},{8,9},{9,10},{10,1... | collective-permute-start | bytes 393224 | tf_op jit(solution)/shard_map/ppermute | solution.py:44
  69.2 6.2 %collective-permute-start.24 = (bf16[128,512]{1,0:T(8,128)(2,1)S(1)}, bf16[128,512]{1,0:T(8,128)(2,1)S(1)}, u32[]{:S(2)}, u32[]{:S(2)}) collective-permute-start(bf16[128,512]{1,0:T(8,128)(2,1)S(1)} %get-tuple-element.44), channel_id=1, source_target_pairs={{0,3},{1,0},{2,1},{3,2},{4,7},{5,4},{6,5},{7,6},{8,11},{9,8},{10,9... | collective-permute-start | bytes 393224 | tf_op jit(solution)/shard_map/ppermute | solution.py:44
  69.3 6.1 %collective-permute-start.17 = (bf16[128,512]{1,0:T(8,128)(2,1)S(1)}, bf16[128,512]{1,0:T(8,128)(2,1)S(1)}, u32[]{:S(2)}, u32[]{:S(2)}) collective-permute-start(bf16[128,512]{1,0:T(8,128)(2,1)S(1)} %add_convert_fusion), channel_id=1, source_target_pairs={{0,16},{16,0},{32,48},{48,32},{64,80},{80,64},{96,112},{112,96},{1... | collective-permute-start | bytes 393224 | tf_op jit(solution)/shard_map/ppermute | solution.py:44
